TPU v7x, 8 devices: a whole 2x2x1 slice. The times are simulated.
8 devices in a mesh: dp: 1 (over z), tp: 8 (over y, x, core).
Axes of the slice: x: 2, y: 2, z: 1, core: 2. Of those that a mesh axis runs over, the one named last changes fastest.
Arguments:
- token_ids: int32 [8192], P('dp')
- positions: int32 [8192], P('dp')
- embed_table: bfloat16 [262144, 2560], P('tp')
- norm_scale: float32 [2560], replicated
- w_query: bfloat16 [2560, 2048], P(None, 'tp')
- w_key: bfloat16 [2560, 1024], replicated
- w_value: bfloat16 [2560, 1024], replicated
Outputs:
- output 1: bfloat16 [8192, 2560], P(('dp', 'tp'))
- output 2: bfloat16 [8192, 8, 256], P('dp', 'tp')
- output 3: bfloat16 [8192, 8, 256], P('dp', 'tp')
- output 4: bfloat16 [8192, 8, 256], P('dp', 'tp')
All inputs are finite; a program needn't handle non-finite values.
Results may differ from a plain program's by a relative error of at most 0.0120427.
Values are sent between devices in bfloat16 or wider.
A program may use at most 1 GiB of HBM per device.

v0:
```python
import math
import jax
import jax.numpy as jnp
from jax import lax
from jax.sharding import PartitionSpec as P

HEAD_DIM = 256
EPSILON = 1e-6
ROPE_BASE = 10000.0


def rope_tables(positions):
    inv_freq = ROPE_BASE ** (-jnp.arange(0, HEAD_DIM, 2, dtype=jnp.float32) / HEAD_DIM)
    angles = positions.astype(jnp.float32)[:, None] * inv_freq[None, :]
    return jnp.cos(angles)[:, None, :], jnp.sin(angles)[:, None, :]


def rotate(head_vals, cosines, sines):
    half_dim = head_vals.shape[-1] // 2
    front_half = head_vals[..., :half_dim]
    back_half = head_vals[..., half_dim:]
    return jnp.concatenate([front_half * cosines - back_half * sines, back_half * cosines + front_half * sines], axis=-1)


def rms_norm(resid_rows, norm_scale):
    widened = resid_rows.astype(jnp.float32)
    inv_rms = lax.rsqrt(jnp.mean(widened * widened, axis=-1, keepdims=True) + EPSILON)
    return (widened * inv_rms * (1.0 + norm_scale)).astype(jnp.bfloat16)


def project(normed, weight, cosines, sines, factor):
    linear = jnp.dot(normed, weight, preferred_element_type=jnp.float32).astype(jnp.bfloat16)
    head_view = linear.reshape(linear.shape[0], -1, HEAD_DIM).astype(jnp.float32)
    return (rotate(head_view, cosines, sines) * factor).astype(jnp.bfloat16)


def solution(mesh):
    group_size = mesh.shape["tp"]

    def local_step(token_ids, positions, table_rows, norm_scale, w_query, w_key, w_value):
        dev_index = lax.axis_index("tp")
        vocab_rows, model_width = table_rows.shape
        normalizer = jnp.asarray(math.sqrt(model_width), dtype=jnp.bfloat16)
        local_ids = token_ids - dev_index * vocab_rows
        inside = (local_ids >= 0) & (local_ids < vocab_rows)
        picked = jnp.take(table_rows, local_ids, axis=0, mode="clip") * normalizer
        partial = jnp.where(inside[:, None], picked, jnp.zeros((), jnp.bfloat16))
        residual = lax.psum_scatter(partial, "tp", scatter_dimension=0, tiled=True)
        normed = lax.all_gather(rms_norm(residual, norm_scale), "tp", axis=0, tiled=True)
        cosines, sines = rope_tables(positions)
        queries = project(normed, w_query, cosines, sines, HEAD_DIM ** -0.5)
        kv_heads = w_key.shape[1] // HEAD_DIM
        slot_count = max(kv_heads, group_size)
        slots_here = slot_count // group_size
        first_head = (dev_index * slots_here) // (slot_count // kv_heads)
        key_cols = lax.dynamic_slice_in_dim(w_key, first_head * HEAD_DIM, slots_here * HEAD_DIM, axis=1)
        value_cols = lax.dynamic_slice_in_dim(w_value, first_head * HEAD_DIM, slots_here * HEAD_DIM, axis=1)
        key_heads = project(normed, key_cols, cosines, sines, 1.0)
        value_lin = jnp.dot(normed, value_cols, preferred_element_type=jnp.float32).astype(jnp.bfloat16)
        value_heads = value_lin.reshape(value_lin.shape[0], slots_here, HEAD_DIM)
        return residual, queries, key_heads, value_heads

    head_spec = P("dp", "tp", None)
    return jax.shard_map(local_step, mesh=mesh, in_specs=(P("dp"), P("dp"), P("tp", None), P(), P(None, "tp"), P(), P()), out_specs=(P(("dp", "tp"), None), head_spec, head_spec, head_spec), check_vma=False)
```

profile of v0, /device:TPU:6, one launch (start us, length us, event | category | flops | bytes accessed | tf_op | source)
XLA Modules:
  0.0 1036.7 jit_solution(11479655831075964211)
XLA Ops:
  7.2 0.0 copy-start
  7.2 0.0 reduce-scatter.4.cloned.1.call-start
  7.2 0.9 compare_and_fusion
  8.1 0.8 subtract_clamp_fusion
  8.9 452.4 %gather_fusion = bf16[8192,2560]{1,0:T(8,128)(2,1)} fusion(bf16[32768,2560]{1,0:T(8,128)(2,1)} %param.9, s32[8192]{0:T(1024)S(1)} %subtract_clamp_fusion), kind=kCustom, calls=%fused_computation | custom fusion | bytes 83918848 | tf_op jit(solution)/shard_map/jit(_take)/gather | solution.py:46
  461.3 28.0 %multiply_select_fusion = bf16[8192,2560]{1,0:T(8,128)(2,1)} fusion(bf16[8192,2560]{1,0:T(8,128)(2,1)} %gather_fusion, pred[8192]{0:T(1024)(128)(4,1)S(1)} %compare_and_fusion), kind=kLoop, calls=%fused_computation.1 | loop fusion | flops 41943040 | bytes 83894272 | tf_op jit(solution)/shard_map/jit(_where)/select_n | solution.py:47
  489.3 0.0 copy-start.3
  489.3 0.0 reduce-scatter.4.cloned.1.call-update
  489.3 0.0 all-gather.2.cloned.1.call-start
  489.4 0.6 copy-done.3
  490.0 238.1 %reduce-scatter.4.cloned.1.call-done = bf16[1024,2560]{1,0:T(8,128)(2,1)} async-done(((bf16[8192,2560]{1,0:T(8,128)(2,1)}), bf16[1024,2560]{1,0:T(8,128)(2,1)}) %reduce-scatter.4.cloned.1.call-update) | async-done | bytes 5242896
  728.1 0.0 copy-start.1
  728.1 3.7 fusion
  731.8 0.3 copy-done.1
  732.1 3.6 fusion.2
  735.7 0.0 copy-start.2
  735.7 0.0 all-gather.2.cloned.1.call-update
  735.8 0.7 copy-done.2
  736.5 191.0 %all-gather.2.cloned.1.call-done = bf16[8192,2560]{1,0:T(8,128)(2,1)} async-done(((bf16[1024,2560]{1,0:T(8,128)(2,1)}), bf16[8192,2560]{1,0:T(8,128)(2,1)}) %all-gather.2.cloned.1.call-update) | async-done | bytes 41943056 | tf_op jit(solution)/shard_map/all_gather | solution.py:49
  927.5 0.0 copy-done
  927.5 21.8 %fusion.4 = f32[8192,1,256]{0,2,1:T(8,128)} fusion(bf16[8192,2560]{1,0:T(8,128)(2,1)} %all-gather.2.cloned.1.call-done, bf16[2560,256]{1,0:T(8,128)(2,1)S(1)} %copy-done), kind=kOutput, calls=%fused_computation.11 | convolution fusion | flops 10741612544 | bytes 51642368 | tf_op jit(solution)/shard_map/dot_general | solution.py:32
  949.3 20.1 %fusion.6 = f32[8192,1,256]{0,2,1:T(8,128)} fusion(bf16[8192,2560]{1,0:T(8,128)(2,1)} %all-gather.2.cloned.1.call-done, bf16[2560,1024]{1,0:T(8,128)(2,1)} %param.12, s32[]{:T(128)S(6)} %select_n.15), kind=kOutput, calls=%fused_computation.13 | convolution fusion | flops 10741612544 | bytes 51642372 | tf_op jit(solution)/shard_map/dot_general | solution.py:32
  969.4 20.2 %fusion.20 = (bf16[8192,1,128]{0,2,1:T(8,128)(2,1)S(1)}, bf16[8192,1,128]{0,2,1:T(8,128)(2,1)S(1)}, f32[8192,1,128]{0,2,1:T(8,128)}, f32[8192,1,128]{0,2,1:T(8,128)}) fusion(f32[8192,1,256]{0,2,1:T(8,128)} %fusion.6, f32[128]{0:T(128)S(1)} %multiply_power_fusion, f32[8192]{0:T(1024)S(1)} %convert_element_type.55, f32[8192,1,256]{0,2,1:T(8,128)} %fusion.4), kind=kLoop, calls=%fused_computation.30 | loop fusion | flops 15728640 | bytes 29393408 | tf_op jit(solution)/shard_map/convert.2
  989.6 2.4 pad_maximum_fusion
  992.0 6.4 copy.14
  998.3 5.1 fusion.8
  1003.4 6.4 copy.13
  1009.8 20.0 %fusion.7 = bf16[8192,1,256]{2,0,1:T(8,128)(2,1)} fusion(bf16[8192,2560]{1,0:T(8,128)(2,1)} %all-gather.2.cloned.1.call-done, bf16[2560,1024]{1,0:T(8,128)(2,1)} %param.13, s32[]{:T(128)S(6)} %select_n.15), kind=kOutput, calls=%fused_computation.14 | convolution fusion | flops 10739515392 | bytes 47448068 | tf_op jit(solution)/shard_map/dot_general | solution.py:59
  (4 shorter events, 0.0 us)
Async XLA Ops:
  7.2 920.3 %copy-start = (bf16[2560,256]{1,0:T(8,128)(2,1)S(1)}, bf16[2560,256]{1,0:T(8,128)(2,1)}, u32[]{:S(2)}) copy-start(bf16[2560,256]{1,0:T(8,128)(2,1)} %param.11) | copy-start | bytes 3932164
  7.2 720.9 %reduce-scatter.4.cloned.1.call-start = ((), (), s32[]{:S(2)}) async-start(), calls=%async_computation.2 | async-start | bytes 47185920
  489.3 0.7 copy-start.3
  489.3 438.1 %all-gather.2.cloned.1.call-start = ((), (), s32[]{:S(2)}) async-start(), calls=%async_computation.1 | async-start | bytes 47185920 | tf_op jit(solution)/shard_map/all_gather | solution.py:49
  728.1 4.0 copy-start.1
  735.7 0.8 copy-start.2
Sparse Core Ops, SparseCore 0:
  489.5 238.5 reduce-scatter.3
  735.9 191.5 all-gather.1
where the time goes:
time: 1050 us; the launch traced here: 1040 us
  local copies, waits for them, and re-layouts  467 us (44%)
  waiting for transfers between devices  429 us (41%)
  other arithmetic  64.6 us (6%)
  matrix products  62 us (6%)
  between operations  14.1 us (1%)
    gather x1, local copies, waits for them, and re-layouts, local_step(): picked = jnp.take(table_rows, local_ids, axis=0, mode='clip') * normalizer  452 us
    unnamed x3, waiting for transfers between devices  238 us
    all_gather x1, waiting for transfers between devices, local_step(): lax.all_gather(rms_norm(residual, norm_scale), 'tp', axis=0, tiled=True)  191 us
    dot_general x2, matrix products, project(): jnp.dot(normed, weight, preferred_element_type=jnp.float32)  41.9 us
    select_n x1, other arithmetic, local_step(): partial = jnp.where(inside[:, None], picked, jnp.zeros((), jnp.bfloat16))  28 us
  transfers between devices with their start and end apart: 2, of which 2 were waited for; matrix products, arithmetic and copies ran while one was open for 0% of the time, Pallas kernels for 0%

commit v1 on v0

v1 whole, which is shorter than its diff:
```python
import functools
import math
import numpy as np
import jax
import jax.numpy as jnp
from jax import lax
from jax.experimental import pallas as pl
from jax.experimental.pallas import tpu as pltpu
from jax.sharding import PartitionSpec as P

HEAD_DIM = 256
EPSILON = 1e-6
ROPE_BASE = 10000.0
MESH = pl.DeviceIdType.MESH

HOT = 1024
CH = 64
CHIP_CHUNKS = (35, 6, 3, 3)
DEV1_CHUNKS = 10
HOT_CHUNKS = HOT // CH
RING_CHUNKS = sum(CHIP_CHUNKS)
RING_ROWS = RING_CHUNKS * CH
ROWS = 2 * RING_ROWS
COLD0_CHUNKS = 2 * CHIP_CHUNKS[0] - DEV1_CHUNKS - HOT_CHUNKS
CAPS = tuple(CH * n for n in (COLD0_CHUNKS, DEV1_CHUNKS, 6, 6, 3, 3, 3, 3))
CAP = max(CAPS)
RING_ORDER = ((0, 1, 3, 2), (0, 2, 3, 1))
BLK = 256
NBLK = -(-RING_ROWS // BLK)
TILE = 128
NTILE = CAP // TILE


def _base_rows():
    base = np.zeros((4, 9), np.int32)
    for chip in range(4):
        for dev in range(9):
            owner, ring = (0, 1) if dev == 8 else (dev // 2, dev % 2)
            order = RING_ORDER[ring]
            pos, src = order.index(chip), order.index(owner)
            hops = (pos - src) % 4
            before = sum(CHIP_CHUNKS[order[(pos - k) % 4]] for k in range(hops))
            base[chip, dev] = ring * RING_ROWS + before * CH
    return base


def _mo(value, step):
    return pl.multiple_of(value, step)


def pack_kernel(flat_ref, par_ref, table, out, pairs, packed, gsem, osem):
    dev = lax.axis_index("tp")
    tiles = jnp.where(dev == 0, NTILE, 0)
    for d in range(1, 8):
        tiles = jnp.where(dev == d, -(-CAPS[d] // TILE), tiles)

    def issue(i):
        def body(j, carry):
            slot = i * TILE + j
            row = flat_ref[slot]
            pltpu.make_async_copy(
                table.at[pl.ds(_mo((row // 2) * 2, 2), 2), :],
                pairs.at[pl.ds(_mo(slot * 2, 2), 2), :], gsem.at[i]).start()
            return carry
        lax.fori_loop(0, TILE, body, 0, unroll=8)

    def out_copy(i):
        here = pl.ds(_mo(i * TILE, TILE), TILE)
        return pltpu.make_async_copy(packed.at[here, :], out.at[here, :], osem.at[i])

    def finish(i):
        both = pl.ds(_mo(i * 2 * TILE, 2 * TILE), 2 * TILE)
        here = pl.ds(_mo(i * TILE, TILE), TILE)
        pltpu.make_async_copy(table.at[pl.ds(0, 2 * TILE), :], pairs.at[both, :], gsem.at[i]).wait()
        row = lax.broadcasted_iota(jnp.int32, (TILE, 2 * TILE), 0)
        col = lax.broadcasted_iota(jnp.int32, (TILE, 2 * TILE), 1)
        pick = jnp.where(col == 2 * row + par_ref[here, :], 1.0, 0.0).astype(jnp.bfloat16)
        packed[here, :] = jnp.dot(pick, pairs[both, :], preferred_element_type=jnp.float32).astype(jnp.bfloat16)
        out_copy(i).start()

    lag = 3

    def step(i, carry):
        @pl.when(i < tiles)
        def _():
            issue(i)

        @pl.when(i >= lag)
        def _():
            finish(i - lag)
        return carry
    lax.fori_loop(0, tiles + lag, step, 0)

    def drain(i, carry):
        out_copy(i).wait()
        return carry
    lax.fori_loop(0, tiles, drain, 0)


def pack_rows(flat, table):
    width = table.shape[1]
    return pl.pallas_call(
        pack_kernel,
        out_shape=jax.ShapeDtypeStruct((CAP, width), jnp.bfloat16),
        in_specs=[pl.BlockSpec(memory_space=pltpu.SMEM), pl.BlockSpec(memory_space=pltpu.VMEM),
                  pl.BlockSpec(memory_space=pl.ANY)],
        out_specs=pl.BlockSpec(memory_space=pl.ANY),
        scratch_shapes=[pltpu.VMEM((2 * CAP, width), jnp.bfloat16), pltpu.VMEM((CAP, width), jnp.bfloat16),
                        pltpu.SemaphoreType.DMA((NTILE,)), pltpu.SemaphoreType.DMA((NTILE,))],
        compiler_params=pltpu.CompilerParams(vmem_limit_bytes=60_000_000),
    )(flat, (flat % 2)[:, None], table)


def ring_kernel(packed, table, idx_ref, scale_ref, wq, wk, wv, lin_out, res_ref,
                rows, acc, wbuf, nbuf, ohbuf, oblk, rsem, nsem, ssem, xsem, osem, wsem):
    width = rows.shape[1]
    tokens = acc.shape[0]
    normalizer = float(np.asarray(math.sqrt(width), dtype=jnp.bfloat16))
    dev = lax.axis_index("tp")
    chip, core = dev // 2, dev % 2
    pos = jnp.where(chip == 0, 0, jnp.where(chip == 3, 2, jnp.where(chip == 1, 1 + 2 * core, 3 - 2 * core)))

    def chip_at(place):
        return jnp.where(place == 0, 0, jnp.where(place == 2, 3, jnp.where(place == 1, 1 + core, 2 - core)))

    def chunks_of(which):
        return jnp.where(which == 0, CHIP_CHUNKS[0], jnp.where(which == 1, CHIP_CHUNKS[1], CHIP_CHUNKS[2]))

    next_chip = chip_at((pos + 1) % 4)
    next_dev = next_chip * 2 + core
    prev_dev = chip_at((pos + 3) % 4) * 2 + core
    sib = chip * 2 + 1 - core
    own = chunks_of(chip)
    n_next = chunks_of(next_chip)
    local = jnp.where(dev == 1, DEV1_CHUNKS, own)
    n_send = RING_CHUNKS - n_next

    barrier = pltpu.get_barrier_semaphore()
    for other in (next_dev, prev_dev, sib):
        pl.semaphore_signal(barrier, inc=1, device_id={"tp": other}, device_id_type=MESH)

    def chunk(ring, i):
        return rows.at[pl.ds(_mo((ring * RING_CHUNKS + i) * CH, CH), CH), :]

    def sem_of(ring, i):
        return rsem.at[ring * RING_CHUNKS + i]

    def wait_chunk(ring, i):
        pltpu.make_async_copy(table.at[pl.ds(0, CH), :], chunk(ring, i), sem_of(ring, i)).wait()

    def to_next(i):
        return pltpu.make_async_remote_copy(
            src_ref=chunk(core, i), dst_ref=chunk(core, i + n_next), send_sem=nsem.at[i],
            recv_sem=sem_of(core, i + n_next), device_id={"tp": next_dev}, device_id_type=MESH)

    def to_sib(i):
        return pltpu.make_async_remote_copy(
            src_ref=chunk(core, i), dst_ref=chunk(core, i), send_sem=ssem.at[i],
            recv_sem=sem_of(core, i), device_id={"tp": sib}, device_id_type=MESH)

    def to_sib_other(i):
        return pltpu.make_async_remote_copy(
            src_ref=chunk(1, i), dst_ref=chunk(1, i), send_sem=xsem.at[i - DEV1_CHUNKS],
            recv_sem=sem_of(1, i), device_id={"tp": sib}, device_id_type=MESH)

    def load(i, carry):
        @pl.when((dev == 0) & (i < HOT_CHUNKS))
        def _():
            pltpu.make_async_copy(table.at[pl.ds(_mo(i * CH, CH), CH), :], chunk(core, i), sem_of(core, i)).start()

        @pl.when((dev != 0) | (i >= HOT_CHUNKS))
        def _():
            first = i - jnp.where(dev == 0, HOT_CHUNKS, 0)
            pltpu.make_async_copy(packed.at[pl.ds(_mo(first * CH, CH), CH), :], chunk(core, i), sem_of(core, i)).start()
        return carry
    lax.fori_loop(0, local, load, 0)

    @pl.when(dev == 0)
    def _():
        def load_other(i, carry):
            first = i - DEV1_CHUNKS + CHIP_CHUNKS[0] - HOT_CHUNKS
            pltpu.make_async_copy(packed.at[pl.ds(_mo(first * CH, CH), CH), :], chunk(1, i), sem_of(1, i)).start()
            return carry
        lax.fori_loop(DEV1_CHUNKS, CHIP_CHUNKS[0], load_other, 0)

    weights = []
    for k, w in enumerate((wq, wk, wv)):
        cols = pl.ds(0, HEAD_DIM) if k == 0 else pl.ds(_mo(chip * HEAD_DIM, HEAD_DIM), HEAD_DIM)
        weights.append(pltpu.make_async_copy(w.at[:, cols], wbuf.at[:, pl.ds(k * HEAD_DIM, HEAD_DIM)], wsem.at[k]))
    for copy in weights:
        copy.start()

    pl.semaphore_wait(barrier, 3)

    def first_sends(i, carry):
        wait_chunk(core, i)
        to_next(i).start()
        return carry
    lax.fori_loop(0, local, first_sends, 0)

    @pl.when(dev == 0)
    def _():
        def send_other(i, carry):
            wait_chunk(1, i)
            to_sib_other(i).start()
            return carry
        lax.fori_loop(DEV1_CHUNKS, CHIP_CHUNKS[0], send_other, 0)

    def first_sib(i, carry):
        to_sib(i).start()
        return carry
    lax.fori_loop(0, local, first_sib, 0)

    acc[...] = jnp.zeros_like(acc)
    for copy in weights:
        copy.wait()

    def relay(i):
        @pl.when((i >= local) & (i < RING_CHUNKS))
        def _():
            wait_chunk(core, i)

            @pl.when(i < n_send)
            def _():
                to_next(i).start()

            @pl.when((dev != 1) | (i >= CHIP_CHUNKS[0]))
            def _():
                to_sib(i).start()

    def lin_copy(first, slot):
        return pltpu.make_async_copy(
            oblk.at[slot], lin_out.at[pl.ds(_mo(first * 8, CH * 8), BLK * 8), :], osem.at[slot])

    def block_start(b):
        return jnp.where(b == NBLK - 1, RING_ROWS - BLK, b * BLK)

    def projections(ring, b, slot, turn):
        first = ring * RING_ROWS + block_start(b)
        gain = 1.0 + scale_ref[...]

        def norm(k, carry):
            emb = rows[pl.ds(_mo(first + k * 32, 32), 32), :].astype(jnp.float32)
            resid = (emb * normalizer).astype(jnp.bfloat16).astype(jnp.float32)
            inv_rms = lax.rsqrt(jnp.mean(resid * resid, axis=-1, keepdims=True) + EPSILON)
            nbuf[pl.ds(_mo(k * 32, 32), 32), :] = (resid * inv_rms * gain).astype(jnp.bfloat16)
            return carry
        lax.fori_loop(0, BLK // 32, norm, 0)

        @pl.when(turn >= 2)
        def _():
            lin_copy(first, slot).wait()
        for k in range(3):
            lin = jnp.dot(nbuf[...], wbuf[:, k * HEAD_DIM:(k + 1) * HEAD_DIM], preferred_element_type=jnp.float32)
            lin = lin.astype(jnp.bfloat16).astype(jnp.float32)
            for half in range(2):
                oblk[slot, pl.ds(2 * k + half, BLK, stride=8), :] = lin[:, half * 128:(half + 1) * 128]
        lin_copy(first, slot).start()

    def pick_tokens(ring, b):
        start = block_start(b)
        first = ring * RING_ROWS + start
        fresh = b * BLK - start
        lane = lax.broadcasted_iota(jnp.int32, (tokens, 128), 1)
        for half in range(2):
            row = lane + half * 128
            hit = (idx_ref[...] - first == row) & (row >= fresh)
            ohbuf[:, half * 128:(half + 1) * 128] = jnp.where(hit, 1.0, 0.0).astype(jnp.bfloat16)

        def part(n, carry):
            cols = pl.ds(_mo(n * 256, 256), 256)
            acc[:, cols] += jnp.dot(ohbuf[...], rows[pl.ds(_mo(first, CH), BLK), cols],
                                    preferred_element_type=jnp.float32)
            return carry
        lax.fori_loop(0, width // 256, part, 0)

    def turn_body(u, carry):
        b, half = u // 2, u % 2
        turn = u - 2
        ring = jnp.where(half == 0, core, 1 - core)
        relay(4 * b + 2 * half)

        @pl.when(turn >= 0)
        def _():
            @pl.when(half == 1)
            def _():
                def wait_one(k, c):
                    i = 4 * (b - 1) + k

                    @pl.when((i < RING_CHUNKS) & ((dev != 0) | (i < DEV1_CHUNKS) | (i >= CHIP_CHUNKS[0])))
                    def _():
                        wait_chunk(1 - core, i)
                    return c
                lax.fori_loop(0, 4, wait_one, 0)
            projections(ring, b - 1, half, turn)
        relay(4 * b + 2 * half + 1)

        @pl.when(turn >= 0)
        def _():
            pick_tokens(ring, b - 1)
        return carry
    lax.fori_loop(0, 2 * NBLK + 2, turn_body, 0)

    def finish(k, carry):
        here = pl.ds(_mo(k * 64, 64), 64)
        res_ref[here, :] = (acc[here, :] * normalizer).astype(jnp.bfloat16)
        return carry
    lax.fori_loop(0, tokens // 64, finish, 0)

    for slot in range(2):
        lin_copy(0, slot).wait()

    def drain_next(i, carry):
        to_next(i).wait_send()
        return carry
    lax.fori_loop(0, n_send, drain_next, 0)

    def drain_sib(i, carry):
        @pl.when((dev != 1) | (i < DEV1_CHUNKS) | (i >= CHIP_CHUNKS[0]))
        def _():
            to_sib(i).wait_send()
        return carry
    lax.fori_loop(0, RING_CHUNKS, drain_sib, 0)

    @pl.when(dev == 0)
    def _():
        def drain_other(i, carry):
            to_sib_other(i).wait_send()
            return carry
        lax.fori_loop(DEV1_CHUNKS, CHIP_CHUNKS[0], drain_other, 0)


def ring_call(packed, table, idx_here, norm_scale, w_query, w_key, w_value):
    width = table.shape[1]
    tokens = idx_here.shape[0]
    anywhere = pl.BlockSpec(memory_space=pl.ANY)
    vmem = pl.BlockSpec(memory_space=pltpu.VMEM)
    return pl.pallas_call(
        ring_kernel,
        out_shape=(jax.ShapeDtypeStruct((ROWS * 8, 128), jnp.float32),
                   jax.ShapeDtypeStruct((tokens, width), jnp.bfloat16)),
        in_specs=[anywhere, anywhere, vmem, vmem, anywhere, anywhere, anywhere],
        out_specs=(anywhere, vmem),
        scratch_shapes=[
            pltpu.VMEM((ROWS, width), jnp.bfloat16),
            pltpu.VMEM((tokens, width), jnp.float32),
            pltpu.VMEM((width, 3 * HEAD_DIM), jnp.bfloat16),
            pltpu.VMEM((BLK, width), jnp.bfloat16),
            pltpu.VMEM((tokens, BLK), jnp.bfloat16),
            pltpu.VMEM((2, BLK * 8, 128), jnp.float32),
            pltpu.SemaphoreType.DMA((2 * RING_CHUNKS,)),
            pltpu.SemaphoreType.DMA((RING_CHUNKS,)),
            pltpu.SemaphoreType.DMA((RING_CHUNKS,)),
            pltpu.SemaphoreType.DMA((CHIP_CHUNKS[0] - DEV1_CHUNKS,)),
            pltpu.SemaphoreType.DMA((2,)),
            pltpu.SemaphoreType.DMA((3,)),
        ],
        compiler_params=pltpu.CompilerParams(collective_id=0, has_side_effects=True, vmem_limit_bytes=67_000_000),
    )(packed, table, jnp.broadcast_to(idx_here[:, None], (tokens, 128)), norm_scale[None, :], w_query, w_key, w_value)


def cos_sin(angle):
    turns = jnp.floor(angle * (2.0 / math.pi) + 0.5)
    rest = ((angle - turns * 1.5703125) - turns * 4.837512969970703125e-4) - turns * 7.54978995489188216e-8
    quarter = turns.astype(jnp.int32)
    z = rest * rest
    s = rest + rest * z * (-1.6666654611e-1 + z * (8.3321608736e-3 + z * -1.9515295891e-4))
    c = 1.0 - 0.5 * z + z * z * (4.166664568298827e-2 + z * (-1.388731625493765e-3 + z * 2.443315711809948e-5))
    odd = (quarter & 1) == 1
    cosine = jnp.where(odd, s, c)
    sine = jnp.where(odd, c, s)
    cosine = jnp.where(((quarter + 1) & 2) == 2, -cosine, cosine)
    sine = jnp.where((quarter & 2) == 2, -sine, sine)
    return cosine, sine


EXPAND = 512
SUB = 64
LOADS = 8


def expand_kernel(idx_ref, pos_ref, freq_ref, lin, q_ref, k_ref, v_ref, table, picked, sem):
    step = pl.program_id(0)
    piece = table.shape[0] // LOADS

    @pl.when(step == 0)
    def _():
        copies = [pltpu.make_async_copy(lin.at[pl.ds(n * piece, piece), :], table.at[pl.ds(n * piece, piece), :],
                                        sem.at[n]) for n in range(LOADS)]
        for copy in copies:
            copy.start()
        for copy in copies:
            copy.wait()

    def take(t, carry):
        row = idx_ref[step * EXPAND + t]
        picked[pl.ds(_mo(t * 8, 8), 8), :] = table[pl.ds(_mo(row * 8, 8), 8), :]
        return carry
    lax.fori_loop(0, EXPAND, take, 0, unroll=16)

    def rope(n, carry):
        here = pl.ds(_mo(n * SUB, SUB), SUB)
        cosines, sines = cos_sin(pos_ref[here, :] * freq_ref[...])
        part = [picked[pl.ds(n * SUB * 8 + s, SUB, stride=8), :] for s in range(6)]
        factor = HEAD_DIM ** -0.5
        q_ref[here, :128] = ((part[0] * cosines - part[1] * sines) * factor).astype(jnp.bfloat16)
        q_ref[here, 128:] = ((part[1] * cosines + part[0] * sines) * factor).astype(jnp.bfloat16)
        k_ref[here, :128] = (part[2] * cosines - part[3] * sines).astype(jnp.bfloat16)
        k_ref[here, 128:] = (part[3] * cosines + part[2] * sines).astype(jnp.bfloat16)
        v_ref[here, :128] = part[4].astype(jnp.bfloat16)
        v_ref[here, 128:] = part[5].astype(jnp.bfloat16)
        return carry
    lax.fori_loop(0, EXPAND // SUB, rope, 0)


def expand(idx, positions, lin):
    tokens = idx.shape[0]
    freq = ROPE_BASE ** (-jnp.arange(0, HEAD_DIM, 2, dtype=jnp.float32) / HEAD_DIM)
    head = jax.ShapeDtypeStruct((tokens, HEAD_DIM), jnp.bfloat16)
    head_spec = pl.BlockSpec((EXPAND, HEAD_DIM), lambda i: (i, 0))
    return pl.pallas_call(
        expand_kernel,
        grid=(tokens // EXPAND,),
        out_shape=(head, head, head),
        in_specs=[pl.BlockSpec(memory_space=pltpu.SMEM), pl.BlockSpec((EXPAND, 1), lambda i: (i, 0)),
                  pl.BlockSpec((1, HEAD_DIM // 2), lambda i: (0, 0)), pl.BlockSpec(memory_space=pl.ANY)],
        out_specs=(head_spec, head_spec, head_spec),
        scratch_shapes=[pltpu.VMEM(lin.shape, jnp.float32), pltpu.VMEM((EXPAND * 8, 128), jnp.float32),
                        pltpu.SemaphoreType.DMA((LOADS,))],
        compiler_params=pltpu.CompilerParams(vmem_limit_bytes=60_000_000),
    )(idx, positions.astype(jnp.float32)[:, None], freq[None, :], lin)


def rope_tables(positions):
    inv_freq = ROPE_BASE ** (-jnp.arange(0, HEAD_DIM, 2, dtype=jnp.float32) / HEAD_DIM)
    angles = positions.astype(jnp.float32)[:, None] * inv_freq[None, :]
    return jnp.cos(angles)[:, None, :], jnp.sin(angles)[:, None, :]


def rotate(head_vals, cosines, sines):
    half_dim = head_vals.shape[-1] // 2
    front_half = head_vals[..., :half_dim]
    back_half = head_vals[..., half_dim:]
    return jnp.concatenate([front_half * cosines - back_half * sines, back_half * cosines + front_half * sines], axis=-1)


def rms_norm(resid_rows, norm_scale):
    widened = resid_rows.astype(jnp.float32)
    inv_rms = lax.rsqrt(jnp.mean(widened * widened, axis=-1, keepdims=True) + EPSILON)
    return (widened * inv_rms * (1.0 + norm_scale)).astype(jnp.bfloat16)


def project(normed, weight, cosines, sines, factor):
    linear = jnp.dot(normed, weight, preferred_element_type=jnp.float32).astype(jnp.bfloat16)
    return (rotate(linear.reshape(linear.shape[0], 1, HEAD_DIM).astype(jnp.float32), cosines, sines) * factor).astype(jnp.bfloat16)


def general(token_ids, positions, table_rows, norm_scale, w_query, w_key, w_value):
    dev = lax.axis_index("tp")
    vocab_rows, width = table_rows.shape
    tokens = token_ids.shape[0]
    normalizer = jnp.asarray(math.sqrt(width), dtype=jnp.bfloat16)
    local_ids = token_ids - dev * vocab_rows
    inside = (local_ids >= 0) & (local_ids < vocab_rows)
    picked = jnp.take(table_rows, local_ids, axis=0, mode="clip") * normalizer
    partial = jnp.where(inside[:, None], picked, jnp.zeros((), jnp.bfloat16))
    parts = lax.all_to_all(partial.reshape(8, tokens // 8, width), "tp", 0, 0)
    residual = jnp.sum(parts.astype(jnp.float32), axis=0).astype(jnp.bfloat16)
    normed = rms_norm(residual, norm_scale)
    normed = lax.all_to_all(jnp.broadcast_to(normed[None], (8,) + normed.shape), "tp", 0, 0).reshape(tokens, width)
    cosines, sines = rope_tables(positions)
    queries = project(normed, w_query, cosines, sines, HEAD_DIM ** -0.5)
    col = (dev // 2) * HEAD_DIM
    key_heads = project(normed, lax.dynamic_slice_in_dim(w_key, col, HEAD_DIM, axis=1), cosines, sines, 1.0)
    value_cols = lax.dynamic_slice_in_dim(w_value, col, HEAD_DIM, axis=1)
    value_heads = jnp.dot(normed, value_cols, preferred_element_type=jnp.float32).astype(jnp.bfloat16)
    return (residual, queries.reshape(tokens, HEAD_DIM), key_heads.reshape(tokens, HEAD_DIM), value_heads)


def solution(mesh):
    base_rows = _base_rows()

    def local_step(token_ids, positions, table_rows, norm_scale, w_query, w_key, w_value):
        dev = lax.axis_index("tp")
        vocab_rows, width = table_rows.shape
        tokens = token_ids.shape[0]
        groups = tokens // 128
        ids = token_ids.reshape(groups, 128)
        owner = ids // vocab_rows
        cold = ids >= HOT
        mine8 = (owner[None] == jnp.arange(8, dtype=jnp.int32)[:, None, None]) & cold[None]
        strict = jnp.asarray(np.triu(np.ones((128, 128)), 1), jnp.bfloat16)
        rank8 = jnp.dot(mine8.astype(jnp.bfloat16).reshape(8 * groups, 128), strict,
                        preferred_element_type=jnp.float32).reshape(8, groups, 128)
        count8 = jnp.sum(mine8.astype(jnp.int32), axis=2)
        offset8 = jnp.sum(jnp.where(np.tri(groups, groups, -1, dtype=bool)[None], count8[:, None, :], 0), axis=2)
        total8 = jnp.sum(count8, axis=1)
        fits = jnp.all(total8 <= jnp.asarray(CAPS, jnp.int32))

        def fast(token_ids, positions, table_rows, norm_scale, w_query, w_key, w_value):
            rank8i = rank8.astype(jnp.int32)
            rank = jnp.sum(jnp.where(mine8, rank8i + offset8[:, :, None], 0), axis=0)
            base = lax.dynamic_index_in_dim(jnp.asarray(base_rows), dev // 2, 0, keepdims=False)
            first = jnp.sum(jnp.where(mine8, base[:8, None, None], 0), axis=0)
            slot0 = jnp.where(cold, HOT + rank, ids)
            split = CHIP_CHUNKS[0] * CH
            idx0 = jnp.where(slot0 < split, base[0] + slot0, base[8] + DEV1_CHUNKS * CH + slot0 - split)
            idx = jnp.where(owner == 0, idx0, first + rank).reshape(tokens)

            mine = lax.dynamic_index_in_dim(mine8, dev, 0, keepdims=False)
            within = lax.dynamic_index_in_dim(rank8i, dev, 0, keepdims=False)
            offset = lax.dynamic_index_in_dim(offset8, dev, 0, keepdims=False)
            count = lax.dynamic_index_in_dim(count8, dev, 0, keepdims=False)
            lane = jnp.arange(128, dtype=jnp.int32)
            place = jnp.where(mine, within, -1)
            local = ids - dev * vocab_rows
            listed = jnp.sum(jnp.where(place[:, None, :] == lane[None, :, None], local[:, None, :], 0), axis=2)
            slot = jnp.arange(CAP, dtype=jnp.int32)[:, None]
            group = (offset[None] <= slot) & (slot < (offset + count)[None])
            digits = jnp.concatenate([listed // 256, listed % 256], axis=1).astype(jnp.bfloat16)
            found = jnp.dot(group.astype(jnp.bfloat16), digits, preferred_element_type=jnp.float32)
            found = (found[:, :128] * 256.0 + found[:, 128:]).astype(jnp.int32)
            column = slot - jnp.sum(jnp.where(group, offset[None], 0), axis=1, keepdims=True)
            flat = jnp.sum(jnp.where(column == lane[None], found, 0), axis=1)

            packed = pack_rows(flat, table_rows)
            share = tokens // 8
            idx_here = lax.dynamic_slice_in_dim(idx, dev * share, share)
            lin, residual = ring_call(packed, table_rows, idx_here, norm_scale, w_query, w_key, w_value)
            queries, key_heads, value_heads = expand(idx, positions, lin)
            return residual, queries, key_heads, value_heads

        outs = lax.cond(fits, fast, general, token_ids, positions, table_rows, norm_scale, w_query, w_key, w_value)
        residual, heads = outs[0], outs[1:]
        return (residual,) + tuple(h.reshape(tokens, 1, HEAD_DIM) for h in heads)

    head_spec = P("dp", "tp", None)
    return jax.shard_map(local_step, mesh=mesh, in_specs=(P("dp"), P("dp"), P("tp", None), P(), P(None, "tp"), P(), P()), out_specs=(P(("dp", "tp"), None), head_spec, head_spec, head_spec), check_vma=False)
```

time: 1050 us -> 298 us (0.28); the launches traced: 1040 us -> 297 us
  local copies, waits for them, and re-layouts: 467 us -> 10.8 us
  waiting for transfers between devices: 429 us -> 0 us
  Pallas kernels: 0 us -> 272 us
  matrix products: 62 us -> 1.55 us
  other arithmetic: 64.6 us -> 10.9 us
  between operations: 14.1 us -> 1.32 us
    gather x1 -> x0, local copies, waits for them, and re-layouts: 452 us -> none  [local_step(): picked = jnp.take(table_rows, local_ids, axis=0, mode='clip') * normalizer]
    pallas_call x0 -> x3, Pallas kernels: none -> 272 us  [the longest x1 219 us: ring_call(): pl.pallas_call(ring_kernel, out_shape=(jax.ShapeDtypeStruct((ROWS * 8, 12...]
    unnamed x3 -> x0, waiting for transfers between devices: 238 us -> none
    all_gather x1 -> x0, waiting for transfers between devices: 191 us -> none  [local_step(): lax.all_gather(rms_norm(residual, norm_scale), 'tp', axis=0, tiled=True)]
    dot_general x3 -> x2, matrix products: 62 us -> 1.55 us  [the longest x1 0.93 us: local_step(): jnp.dot(mine8.astype(jnp.bfloat16).reshape(8 * groups, 128), strict, pref...]
    select_n x1 -> x2, other arithmetic: 28 us -> 2.16 us  [the longest x1 2.15 us: pack_rows(): flat % 2]
    another operation x1, other arithmetic: 20.2 us -> 0.04 us
  transfers between devices with their start and end apart: 2 -> 0, of which waited for: 2 -> 0; matrix products, arithmetic and copies ran while one was open for 0% -> 0% of each run, Pallas kernels for 0% -> 0%
where the time goes in v1:
time: 298 us; the launch traced here: 297 us
  Pallas kernels  272 us (91%)
  other arithmetic  10.9 us (4%)
  local copies, waits for them, and re-layouts  10.8 us (4%)
    pallas_call x1, Pallas kernels, ring_call(): pl.pallas_call(ring_kernel, out_shape=(jax.ShapeDtypeStruct((ROWS * 8, 12...  219 us
    pallas_call x1, Pallas kernels, expand(): pl.pallas_call(expand_kernel, grid=(tokens // EXPAND,), out_shape=(head,...  42.6 us
    pallas_call x1, Pallas kernels, pack_rows(): pl.pallas_call(pack_kernel, out_shape=jax.ShapeDtypeStruct((CAP, width),...  9.86 us

profile of v1, /device:TPU:6, one launch (start us, length us, event | category | flops | bytes accessed | tf_op | source)
XLA Modules:
  0.0 297.4 jit_solution(5857320305471457203)
XLA Ops:
  0.6 0.8 negate_select_fusion.5
  1.4 0.8 broadcast_compare_fusion.1
  2.2 0.9 fusion.57
  3.2 0.2 convert_reduce_fusion
  3.4 1.3 compare_reduce_fusion
  5.4 286.8 %conditional.1 = (bf16[1024,2560]{1,0:T(8,128)(2,1)}, bf16[8192,1,256]{2,0,1:T(8,128)(2,1)}, bf16[8192,1,256]{2,0,1:T(8,128)(2,1)}, bf16[8192,1,256]{2,0,1:T(8,128)(2,1)}) conditional(s32[]{:T(128)} %convert_element_type.79, (s32[8192]{0:T(1024)}, bf16[32768,2560]{1,0:T(8,128)(2,1)}, f32[2560]{0:T(1024)}, bf16[2560,256]{1,0:T(8,128)(2,1)}, ...), branch_computations={%region_2.5_spmd, %region_5.13_spmd} | conditional | flops 32331853824 | bytes 857955456 | solution.py:533
  5.7 0.7 constant_dynamic-slice_fusion
  6.4 0.2 reduce_sum.88
  6.6 0.9 select_reduce_fusion.4
  7.5 0.2 select_reduce_fusion.3
  7.7 0.6 fusion.60
  8.9 1.4 select_bitcast_fusion
  10.3 0.0 copy-start.2
  10.4 1.7 select_reduce_fusion
  12.2 0.6 fusion.8
  12.8 0.2 select_reduce_fusion.1
  13.0 0.4 fusion.5.flat_ref
  13.4 0.0 copy-start.5
  13.4 2.1 add_select_fusion.par_ref
  15.5 0.0 copy-done.5
  15.5 0.0 copy-start.7
  15.5 9.9 %branch_1_fun.3.packed = bf16[2816,2560]{1,0:T(8,128)(2,1)} custom-call(s32[2816]{0:T(1024)} %copy-done.5, s32[2816,1]{1,0:T(8,128)} %add_select_fusion.par_ref, bf16[32768,2560]{1,0:T(8,128)(2,1)} %get-tuple-element.94.table), custom_call_target="tpu_custom_call" | custom-call | tf_op jit(solution)/shard_map/cond/branch_1_fun/pallas_call | solution.py:102
  25.4 0.0 copy-done.2
  25.4 1.0 broadcast_in_dim.131.idx_ref
  26.4 0.0 copy-done.7
  26.4 0.6 broadcast_in_dim.132.scale_ref
  27.0 0.0 copy-start.4
  27.0 219.2 %branch_1_fun.4 = (f32[48128,128]{1,0:T(8,128)}, bf16[1024,2560]{1,0:T(8,128)(2,1)}) custom-call(bf16[2816,2560]{1,0:T(8,128)(2,1)} %branch_1_fun.3.packed, bf16[32768,2560]{1,0:T(8,128)(2,1)} %get-tuple-element.94.table, s32[1024,128]{1,0:T(8,128)} %broadcast_in_dim.131.idx_ref, f32[1,2560]{1,0:T(1,128)} %broadcast_in_dim.132.scale_ref, ...), custom_call_target="tpu_custom_call" | custom-call | tf_op jit(solution)/shard_map/cond/branch_1_fun/pallas_call | solution.py:338
  246.3 0.0 copy-done.4
  246.3 2.7 copy.36.pos_ref
  249.0 0.5 multiply_power_fusion.freq_ref
  249.5 42.6 %branch_1_fun.5 = (bf16[8192,256]{1,0:T(8,128)(2,1)}, bf16[8192,256]{1,0:T(8,128)(2,1)}, bf16[8192,256]{1,0:T(8,128)(2,1)}) custom-call(s32[8192]{0:T(1024)} %copy-done.2, f32[8192,1]{1,0:T(8,128)} %copy.36.pos_ref, f32[1,128]{1,0:T(1,128)} %multiply_power_fusion.freq_ref, f32[48128,128]{1,0:T(8,128)} %get-tuple-element.106.lin), custom_call_target="tpu_custom_call" | custom-call | tf_op jit(solution)/shard_map/cond/branch_1_fun/pallas_call | solution.py:421
  292.2 5.2 %copy.48 = bf16[1024,2560]{1,0:T(8,128)(2,1)} copy(bf16[1024,2560]{1,0:T(8,128)(2,1)} %get-tuple-element.169) | data formatting | bytes 10485760
  (10 shorter events, 0.2 us)
Async XLA Ops:
  10.3 15.1 %copy-start.2 = (s32[8192]{0:T(1024)}, s32[8192]{0:T(1024)S(1)}, u32[]{:S(2)}) copy-start(s32[8192]{0:T(1024)S(1)} %get-tuple-element.136.idx_ref) | copy-start | bytes 98308 | tf_op jit(solution)/shard_map/cond
  13.4 2.2 copy-start.5
  15.5 10.9 %copy-start.7 = (f32[2560]{0:T(1024)S(1)}, f32[2560]{0:T(1024)}, u32[]{:S(2)}) copy-start(f32[2560]{0:T(1024)} %get-tuple-element.100) | copy-start | bytes 30724 | tf_op jit(solution)/shard_map/cond
  27.0 219.3 %copy-start.4 = (s32[8192]{0:T(1024)S(1)}, s32[8192]{0:T(1024)}, u32[]{:S(2)}) copy-start(s32[8192]{0:T(1024)} %get-tuple-element.105) | copy-start | bytes 98308 | tf_op jit(solution)/shard_map/cond

commit v2 on v1

--- a/solution.py
+++ b/solution.py
@@ -25,7 +25,7 @@
 CAPS = tuple(CH * n for n in (COLD0_CHUNKS, DEV1_CHUNKS, 6, 6, 3, 3, 3, 3))
 CAP = max(CAPS)
 RING_ORDER = ((0, 1, 3, 2), (0, 2, 3, 1))
-BLK = 256
+BLK = 128
 NBLK = -(-RING_ROWS // BLK)
 TILE = 128
 NTILE = CAP // TILE
@@ -48,21 +48,33 @@
     return pl.multiple_of(value, step)
 
 
-def pack_kernel(flat_ref, par_ref, table, out, pairs, packed, gsem, osem):
+def start_pairs(count, row_of, source, pairs, first, sem):
+    def body(j, carry):
+        into = pairs.at[pl.ds(_mo(first + 16 * j, 16), 16), :]
+        for k in range(8):
+            even = row_of(8 * j + k) & -2
+            pltpu.make_async_copy(
+                source.at[pl.ds(_mo(even, 2), 2), :], into.at[pl.ds(2 * k, 2), :], sem).start(priority=k % 2)
+        return carry
+    lax.fori_loop(0, count // 8, body, 0)
+
+
+def pick_odd(rows_row, count):
+    odd = jnp.transpose(jnp.broadcast_to(rows_row & 1, (128, 128)))[:count, :]
+    row = lax.broadcasted_iota(jnp.int32, (count, 128), 0)
+    col = lax.broadcasted_iota(jnp.int32, (count, 128), 1)
+    halves = [jnp.where(col + part == 2 * row + odd, 1.0, 0.0) for part in range(0, 2 * count, 128)]
+    return jnp.concatenate(halves, axis=1).astype(jnp.bfloat16)
+
+
+def pack_kernel(flat_ref, rows_ref, table, out, pairs, packed, gsem, osem):
     dev = lax.axis_index("tp")
     tiles = jnp.where(dev == 0, NTILE, 0)
     for d in range(1, 8):
         tiles = jnp.where(dev == d, -(-CAPS[d] // TILE), tiles)
 
     def issue(i):
-        def body(j, carry):
-            slot = i * TILE + j
-            row = flat_ref[slot]
-            pltpu.make_async_copy(
-                table.at[pl.ds(_mo((row // 2) * 2, 2), 2), :],
-                pairs.at[pl.ds(_mo(slot * 2, 2), 2), :], gsem.at[i]).start()
-            return carry
-        lax.fori_loop(0, TILE, body, 0, unroll=8)
+        start_pairs(TILE, lambda j: flat_ref[i * TILE + j], table, pairs, i * 2 * TILE, gsem.at[i])
 
     def out_copy(i):
         here = pl.ds(_mo(i * TILE, TILE), TILE)
@@ -72,9 +84,7 @@
         both = pl.ds(_mo(i * 2 * TILE, 2 * TILE), 2 * TILE)
         here = pl.ds(_mo(i * TILE, TILE), TILE)
         pltpu.make_async_copy(table.at[pl.ds(0, 2 * TILE), :], pairs.at[both, :], gsem.at[i]).wait()
-        row = lax.broadcasted_iota(jnp.int32, (TILE, 2 * TILE), 0)
-        col = lax.broadcasted_iota(jnp.int32, (TILE, 2 * TILE), 1)
-        pick = jnp.where(col == 2 * row + par_ref[here, :], 1.0, 0.0).astype(jnp.bfloat16)
+        pick = pick_odd(rows_ref[pl.ds(i, 1), :], TILE)
         packed[here, :] = jnp.dot(pick, pairs[both, :], preferred_element_type=jnp.float32).astype(jnp.bfloat16)
         out_copy(i).start()
 
@@ -108,13 +118,12 @@
         scratch_shapes=[pltpu.VMEM((2 * CAP, width), jnp.bfloat16), pltpu.VMEM((CAP, width), jnp.bfloat16),
                         pltpu.SemaphoreType.DMA((NTILE,)), pltpu.SemaphoreType.DMA((NTILE,))],
         compiler_params=pltpu.CompilerParams(vmem_limit_bytes=60_000_000),
-    )(flat, (flat % 2)[:, None], table)
-
-
-def ring_kernel(packed, table, idx_ref, scale_ref, wq, wk, wv, lin_out, res_ref,
-                rows, acc, wbuf, nbuf, ohbuf, oblk, rsem, nsem, ssem, xsem, osem, wsem):
+    )(flat, flat.reshape(NTILE, TILE), table)
+
+
+def ring_kernel(packed, table, pos_ref, freq_ref, scale_ref, wq, wk, wv, lin_out, rows_out, rope_out,
+                rows, wbuf, nbuf, oblk, rope_buf, rsem, nsem, ssem, xsem, osem, ksem, psem, wsem):
     width = rows.shape[1]
-    tokens = acc.shape[0]
     normalizer = float(np.asarray(math.sqrt(width), dtype=jnp.bfloat16))
     dev = lax.axis_index("tp")
     chip, core = dev // 2, dev % 2
@@ -211,7 +220,6 @@
         return carry
     lax.fori_loop(0, local, first_sib, 0)
 
-    acc[...] = jnp.zeros_like(acc)
     for copy in weights:
         copy.wait()
 
@@ -231,6 +239,25 @@
     def lin_copy(first, slot):
         return pltpu.make_async_copy(
             oblk.at[slot], lin_out.at[pl.ds(_mo(first * 8, CH * 8), BLK * 8), :], osem.at[slot])
+
+    def keep_copy(first, slot):
+        here = pl.ds(_mo(first, CH), BLK)
+        return pltpu.make_async_copy(rows.at[here, :], rows_out.at[here, :], ksem.at[slot])
+
+    def rope_copy(group, slot):
+        return pltpu.make_async_copy(
+            rope_buf.at[slot], rope_out.at[pl.ds(_mo(group * 128, 128), 128), :], psem.at[slot])
+
+    def rope_tables_of(group, slot):
+        angle = jnp.transpose(jnp.broadcast_to(pos_ref[pl.ds(group, 1), :], (128, 128))) * freq_ref[...]
+        cosine, sine = cos_sin(angle)
+
+        @pl.when(group >= 2)
+        def _():
+            rope_copy(group, slot).wait()
+        rope_buf[slot, :, :128] = cosine
+        rope_buf[slot, :, 128:] = sine
+        rope_copy(group, slot).start()
 
     def block_start(b):
         return jnp.where(b == NBLK - 1, RING_ROWS - BLK, b * BLK)
@@ -250,6 +277,8 @@
         @pl.when(turn >= 2)
         def _():
             lin_copy(first, slot).wait()
+            keep_copy(first, slot).wait()
+        keep_copy(first, slot).start()
         for k in range(3):
             lin = jnp.dot(nbuf[...], wbuf[:, k * HEAD_DIM:(k + 1) * HEAD_DIM], preferred_element_type=jnp.float32)
             lin = lin.astype(jnp.bfloat16).astype(jnp.float32)
@@ -257,58 +286,37 @@
                 oblk[slot, pl.ds(2 * k + half, BLK, stride=8), :] = lin[:, half * 128:(half + 1) * 128]
         lin_copy(first, slot).start()
 
-    def pick_tokens(ring, b):
-        start = block_start(b)
-        first = ring * RING_ROWS + start
-        fresh = b * BLK - start
-        lane = lax.broadcasted_iota(jnp.int32, (tokens, 128), 1)
-        for half in range(2):
-            row = lane + half * 128
-            hit = (idx_ref[...] - first == row) & (row >= fresh)
-            ohbuf[:, half * 128:(half + 1) * 128] = jnp.where(hit, 1.0, 0.0).astype(jnp.bfloat16)
-
-        def part(n, carry):
-            cols = pl.ds(_mo(n * 256, 256), 256)
-            acc[:, cols] += jnp.dot(ohbuf[...], rows[pl.ds(_mo(first, CH), BLK), cols],
-                                    preferred_element_type=jnp.float32)
-            return carry
-        lax.fori_loop(0, width // 256, part, 0)
-
     def turn_body(u, carry):
         b, half = u // 2, u % 2
         turn = u - 2
         ring = jnp.where(half == 0, core, 1 - core)
-        relay(4 * b + 2 * half)
+        relay(u)
 
         @pl.when(turn >= 0)
         def _():
             @pl.when(half == 1)
             def _():
                 def wait_one(k, c):
-                    i = 4 * (b - 1) + k
+                    i = 2 * (b - 1) + k
 
                     @pl.when((i < RING_CHUNKS) & ((dev != 0) | (i < DEV1_CHUNKS) | (i >= CHIP_CHUNKS[0])))
                     def _():
                         wait_chunk(1 - core, i)
                     return c
-                lax.fori_loop(0, 4, wait_one, 0)
+                lax.fori_loop(0, 2, wait_one, 0)
             projections(ring, b - 1, half, turn)
-        relay(4 * b + 2 * half + 1)
-
-        @pl.when(turn >= 0)
-        def _():
-            pick_tokens(ring, b - 1)
+
+        @pl.when((b >= 2) & (b < 2 + pos_ref.shape[0] // 4))
+        def _():
+            for k in range(2):
+                rope_tables_of((u - 4) * 2 + k, k)
         return carry
     lax.fori_loop(0, 2 * NBLK + 2, turn_body, 0)
-
-    def finish(k, carry):
-        here = pl.ds(_mo(k * 64, 64), 64)
-        res_ref[here, :] = (acc[here, :] * normalizer).astype(jnp.bfloat16)
-        return carry
-    lax.fori_loop(0, tokens // 64, finish, 0)
 
     for slot in range(2):
         lin_copy(0, slot).wait()
+        keep_copy(0, slot).wait()
+        rope_copy(0, slot).wait()
 
     def drain_next(i, carry):
         to_next(i).wait_send()
@@ -330,33 +338,37 @@
         lax.fori_loop(DEV1_CHUNKS, CHIP_CHUNKS[0], drain_other, 0)
 
 
-def ring_call(packed, table, idx_here, norm_scale, w_query, w_key, w_value):
+def ring_call(packed, table, positions, norm_scale, w_query, w_key, w_value):
     width = table.shape[1]
-    tokens = idx_here.shape[0]
+    tokens = positions.shape[0]
+    freq = ROPE_BASE ** (-jnp.arange(0, HEAD_DIM, 2, dtype=jnp.float32) / HEAD_DIM)
     anywhere = pl.BlockSpec(memory_space=pl.ANY)
     vmem = pl.BlockSpec(memory_space=pltpu.VMEM)
     return pl.pallas_call(
         ring_kernel,
         out_shape=(jax.ShapeDtypeStruct((ROWS * 8, 128), jnp.float32),
-                   jax.ShapeDtypeStruct((tokens, width), jnp.bfloat16)),
-        in_specs=[anywhere, anywhere, vmem, vmem, anywhere, anywhere, anywhere],
-        out_specs=(anywhere, vmem),
+                   jax.ShapeDtypeStruct((ROWS, width), jnp.bfloat16),
+                   jax.ShapeDtypeStruct((tokens, HEAD_DIM), jnp.float32)),
+        in_specs=[anywhere, anywhere, vmem, vmem, vmem, anywhere, anywhere, anywhere],
+        out_specs=(anywhere, anywhere, anywhere),
         scratch_shapes=[
             pltpu.VMEM((ROWS, width), jnp.bfloat16),
-            pltpu.VMEM((tokens, width), jnp.float32),
             pltpu.VMEM((width, 3 * HEAD_DIM), jnp.bfloat16),
             pltpu.VMEM((BLK, width), jnp.bfloat16),
-            pltpu.VMEM((tokens, BLK), jnp.bfloat16),
             pltpu.VMEM((2, BLK * 8, 128), jnp.float32),
+            pltpu.VMEM((2, 128, HEAD_DIM), jnp.float32),
             pltpu.SemaphoreType.DMA((2 * RING_CHUNKS,)),
             pltpu.SemaphoreType.DMA((RING_CHUNKS,)),
             pltpu.SemaphoreType.DMA((RING_CHUNKS,)),
             pltpu.SemaphoreType.DMA((CHIP_CHUNKS[0] - DEV1_CHUNKS,)),
             pltpu.SemaphoreType.DMA((2,)),
+            pltpu.SemaphoreType.DMA((2,)),
+            pltpu.SemaphoreType.DMA((2,)),
             pltpu.SemaphoreType.DMA((3,)),
         ],
-        compiler_params=pltpu.CompilerParams(collective_id=0, has_side_effects=True, vmem_limit_bytes=67_000_000),
-    )(packed, table, jnp.broadcast_to(idx_here[:, None], (tokens, 128)), norm_scale[None, :], w_query, w_key, w_value)
+        compiler_params=pltpu.CompilerParams(collective_id=0, has_side_effects=True, vmem_limit_bytes=60_000_000),
+    )(packed, table, positions.astype(jnp.float32).reshape(tokens // 128, 128), freq[None, :], norm_scale[None, :],
+      w_query, w_key, w_value)
 
 
 def cos_sin(angle):
@@ -376,32 +388,44 @@
 
 EXPAND = 512
 SUB = 64
+SHARE = 64
 LOADS = 8
 
 
-def expand_kernel(idx_ref, pos_ref, freq_ref, lin, q_ref, k_ref, v_ref, table, picked, sem):
-    step = pl.program_id(0)
+def expand_kernel(idx_ref, here_ref, rope_ref, lin, rows, res_ref, q_ref, k_ref, v_ref,
+                  table, even, odd, pairs, sem, gsem):
+    step, steps = pl.program_id(0), pl.num_programs(0)
+    first = lax.axis_index("tp") * (steps * SHARE)
     piece = table.shape[0] // LOADS
+    tiles = EXPAND // SUB
+    last = steps * tiles - 1
+
+    def start_share(n):
+        start_pairs(SHARE, lambda j: idx_ref[first + n * SHARE + j], rows, pairs, n * 2 * SHARE, gsem.at[n])
+
+    def take(tile, picked):
+        for t in range(SUB):
+            row = idx_ref[tile * SUB + t]
+            picked[8 * t:8 * t + 8, :] = table[pl.ds(_mo(row * 8, 8), 8), :]
 
     @pl.when(step == 0)
     def _():
         copies = [pltpu.make_async_copy(lin.at[pl.ds(n * piece, piece), :], table.at[pl.ds(n * piece, piece), :],
                                         sem.at[n]) for n in range(LOADS)]
-        for copy in copies:
-            copy.start()
+        for n, copy in enumerate(copies):
+            copy.start(priority=n % 2)
+        def start_one(n, carry):
+            start_share(n)
+            return carry
+        lax.fori_loop(0, steps, start_one, 0)
         for copy in copies:
             copy.wait()
-
-    def take(t, carry):
-        row = idx_ref[step * EXPAND + t]
-        picked[pl.ds(_mo(t * 8, 8), 8), :] = table[pl.ds(_mo(row * 8, 8), 8), :]
-        return carry
-    lax.fori_loop(0, EXPAND, take, 0, unroll=16)
-
-    def rope(n, carry):
+        take(0, even)
+
+    def rope(n, picked):
         here = pl.ds(_mo(n * SUB, SUB), SUB)
-        cosines, sines = cos_sin(pos_ref[here, :] * freq_ref[...])
-        part = [picked[pl.ds(n * SUB * 8 + s, SUB, stride=8), :] for s in range(6)]
+        cosines, sines = rope_ref[here, :128], rope_ref[here, 128:]
+        part = [picked[pl.ds(s, SUB, stride=8), :] for s in range(6)]
         factor = HEAD_DIM ** -0.5
         q_ref[here, :128] = ((part[0] * cosines - part[1] * sines) * factor).astype(jnp.bfloat16)
         q_ref[here, 128:] = ((part[1] * cosines + part[0] * sines) * factor).astype(jnp.bfloat16)
@@ -409,26 +433,42 @@
         k_ref[here, 128:] = (part[3] * cosines + part[2] * sines).astype(jnp.bfloat16)
         v_ref[here, :128] = part[4].astype(jnp.bfloat16)
         v_ref[here, 128:] = part[5].astype(jnp.bfloat16)
-        return carry
-    lax.fori_loop(0, EXPAND // SUB, rope, 0)
-
-
-def expand(idx, positions, lin):
-    tokens = idx.shape[0]
-    freq = ROPE_BASE ** (-jnp.arange(0, HEAD_DIM, 2, dtype=jnp.float32) / HEAD_DIM)
+
+    def two_tiles(n, carry):
+        tile = step * tiles + 2 * n
+        take(tile + 1, odd)
+        rope(2 * n, even)
+        take(jnp.minimum(tile + 2, last), even)
+        rope(2 * n + 1, odd)
+        return carry
+    lax.fori_loop(0, tiles // 2, two_tiles, 0)
+
+    share = pairs.at[pl.ds(_mo(step * 2 * SHARE, 2 * SHARE), 2 * SHARE), :]
+    pltpu.make_async_copy(rows.at[pl.ds(0, 2 * SHARE), :], share, gsem.at[step]).wait()
+    normalizer = float(np.asarray(math.sqrt(rows.shape[1]), dtype=jnp.bfloat16))
+    half = jnp.where(step % 2 == 0, here_ref[pl.ds(step // 2, 1), :], pltpu.roll(here_ref[pl.ds(step // 2, 1), :], 128 - SHARE, 1))
+    emb = jnp.dot(pick_odd(half, SHARE), share[...], preferred_element_type=jnp.float32)
+    res_ref[...] = (emb * normalizer).astype(jnp.bfloat16)
+
+
+def expand(idx, idx_here, rope, lin, rows):
+    tokens, width = idx.shape[0], rows.shape[1]
+    steps = tokens // EXPAND
     head = jax.ShapeDtypeStruct((tokens, HEAD_DIM), jnp.bfloat16)
     head_spec = pl.BlockSpec((EXPAND, HEAD_DIM), lambda i: (i, 0))
     return pl.pallas_call(
         expand_kernel,
-        grid=(tokens // EXPAND,),
-        out_shape=(head, head, head),
-        in_specs=[pl.BlockSpec(memory_space=pltpu.SMEM), pl.BlockSpec((EXPAND, 1), lambda i: (i, 0)),
-                  pl.BlockSpec((1, HEAD_DIM // 2), lambda i: (0, 0)), pl.BlockSpec(memory_space=pl.ANY)],
-        out_specs=(head_spec, head_spec, head_spec),
-        scratch_shapes=[pltpu.VMEM(lin.shape, jnp.float32), pltpu.VMEM((EXPAND * 8, 128), jnp.float32),
-                        pltpu.SemaphoreType.DMA((LOADS,))],
+        grid=(steps,),
+        out_shape=(jax.ShapeDtypeStruct((steps * SHARE, width), jnp.bfloat16), head, head, head),
+        in_specs=[pl.BlockSpec(memory_space=pltpu.SMEM), pl.BlockSpec(memory_space=pltpu.VMEM),
+                  pl.BlockSpec((EXPAND, HEAD_DIM), lambda i: (i, 0)),
+                  pl.BlockSpec(memory_space=pl.ANY), pl.BlockSpec(memory_space=pl.ANY)],
+        out_specs=(pl.BlockSpec((SHARE, width), lambda i: (i, 0)), head_spec, head_spec, head_spec),
+        scratch_shapes=[pltpu.VMEM(lin.shape, jnp.float32), pltpu.VMEM((SUB * 8, 128), jnp.float32),
+                        pltpu.VMEM((SUB * 8, 128), jnp.float32), pltpu.VMEM((steps * 2 * SHARE, width), jnp.bfloat16),
+                        pltpu.SemaphoreType.DMA((LOADS,)), pltpu.SemaphoreType.DMA((steps,))],
         compiler_params=pltpu.CompilerParams(vmem_limit_bytes=60_000_000),
-    )(idx, positions.astype(jnp.float32)[:, None], freq[None, :], lin)
+    )(idx, idx_here.reshape(-1, 128), rope, lin, rows)
 
 
 def rope_tables(positions):
@@ -526,9 +566,8 @@
             packed = pack_rows(flat, table_rows)
             share = tokens // 8
             idx_here = lax.dynamic_slice_in_dim(idx, dev * share, share)
-            lin, residual = ring_call(packed, table_rows, idx_here, norm_scale, w_query, w_key, w_value)
-            queries, key_heads, value_heads = expand(idx, positions, lin)
-            return residual, queries, key_heads, value_heads
+            lin, rows, rope = ring_call(packed, table_rows, positions, norm_scale, w_query, w_key, w_value)
+            return tuple(expand(idx, idx_here, rope, lin, rows))
 
         outs = lax.cond(fits, fast, general, token_ids, positions, table_rows, norm_scale, w_query, w_key, w_value)
         residual, heads = outs[0], outs[1:]

time: 298 us -> 247 us (0.83)
  Pallas kernels: 272 us -> 229 us
  local copies, waits for them, and re-layouts: 10.8 us -> 2.52 us
    pallas_call x1, Pallas kernels: 219 us -> 189 us  [ring_call(): pl.pallas_call(ring_kernel, out_shape=(jax.ShapeDtypeStruct((ROWS * 8, 12...]
    pallas_call x1, Pallas kernels: 42.6 us -> 31.1 us  [expand(): pl.pallas_call(expand_kernel, grid=(steps,), out_shape=(jax.ShapeDtypeStr...]
    unnamed x1 -> x0, local copies, waits for them, and re-layouts: 5.18 us -> none
    broadcast_in_dim x2 -> x0, local copies, waits for them, and re-layouts: 3.68 us -> none  [the longest x1 2.68 us: expand(): positions.astype(jnp.float32)[:, None]]
where the time goes in v2:
time: 247 us; the launch traced here: 246 us
  Pallas kernels  229 us (93%)
  other arithmetic  9.95 us (4%)
  local copies, waits for them, and re-layouts  2.52 us (1%)
    pallas_call x1, Pallas kernels, ring_call(): pl.pallas_call(ring_kernel, out_shape=(jax.ShapeDtypeStruct((ROWS * 8, 12...  189 us
    pallas_call x1, Pallas kernels, expand(): pl.pallas_call(expand_kernel, grid=(steps,), out_shape=(jax.ShapeDtypeStr...  31.1 us
    pallas_call x1, Pallas kernels, pack_rows(): pl.pallas_call(pack_kernel, out_shape=jax.ShapeDtypeStruct((CAP, width),...  9 us

profile of v2, /device:TPU:6, one launch (start us, length us, event | category | flops | bytes accessed | tf_op | source)
XLA Modules:
  0.0 245.6 jit_solution(4548293963882465135)
XLA Ops:
  0.6 0.8 negate_select_fusion.4
  1.4 0.8 broadcast_compare_fusion.1
  2.2 0.9 fusion.53
  3.2 0.2 convert_reduce_fusion
  3.4 1.3 compare_reduce_fusion
  5.4 240.0 %conditional.1 = (bf16[1024,2560]{1,0:T(8,128)(2,1)}, bf16[8192,1,256]{2,0,1:T(8,128)(2,1)}, bf16[8192,1,256]{2,0,1:T(8,128)(2,1)}, bf16[8192,1,256]{2,0,1:T(8,128)(2,1)}) conditional(s32[]{:T(128)} %convert_element_type.79, (s32[8192]{0:T(1024)}, bf16[32768,2560]{1,0:T(8,128)(2,1)}, f32[2560]{0:T(1024)}, bf16[2560,256]{1,0:T(8,128)(2,1)}, ...), branch_computations={%region_2.5_spmd, %region_5.13_spmd} | conditional | flops 32331853824 | bytes 857955456 | solution.py:572
  5.7 0.7 constant_dynamic-slice_fusion.2
  6.4 0.2 reduce_sum.87
  6.6 0.9 select_reduce_fusion.4
  7.5 0.2 select_reduce_fusion.3
  7.7 0.6 fusion.56
  8.9 1.4 broadcast_subtract_fusion
  10.3 0.0 copy-start.3
  10.4 1.7 select_reduce_fusion
  12.2 0.6 fusion.4
  12.8 0.2 select_reduce_fusion.1
  13.0 0.0 slice-start
  13.0 1.0 fusion.2.flat_ref
  14.0 0.0 copy-start.5
  14.0 0.0 copy-start.7
  14.0 0.0 slice-start.1
  14.0 0.0 copy-start.2
  14.0 9.0 %branch_1_fun.3.packed = bf16[2816,2560]{1,0:T(8,128)(2,1)} custom-call(s32[2816]{0:T(1024)} %fusion.2.flat_ref, s32[22,128]{1,0:T(8,128)} %bitcast.53, bf16[32768,2560]{1,0:T(8,128)(2,1)} %get-tuple-element.103.table), custom_call_target="tpu_custom_call" | custom-call | tf_op jit(solution)/shard_map/cond/branch_1_fun/pallas_call | solution.py:112
  23.0 0.0 copy-done.5
  23.0 0.6 convert_bitcast_fusion.pos_ref
  23.6 0.0 copy-done.7
  23.6 0.6 broadcast_in_dim.123.scale_ref
  24.2 0.5 multiply_power_fusion.freq_ref
  24.7 0.0 slice-done
  24.8 0.0 slice-done.1
  24.8 0.0 copy-done.2
  24.8 188.9 %branch_1_fun.4 = (f32[48128,128]{1,0:T(8,128)}, bf16[6016,2560]{1,0:T(8,128)(2,1)}, f32[8192,256]{1,0:T(8,128)}) custom-call(bf16[2816,2560]{1,0:T(8,128)(2,1)} %branch_1_fun.3.packed, bf16[32768,2560]{1,0:T(8,128)(2,1)} %get-tuple-element.103.table, f32[64,128]{1,0:T(8,128)} %convert_bitcast_fusion.pos_ref, f32[1,128]{1,0:T(1,128)} %multiply_power_fusion.freq_ref, ...), custom_call_target="tpu_custom_call" | custom-call | tf_op jit(solution)/shard_map/cond/branch_1_fun/pallas_call | solution.py:347
  213.7 0.0 copy-done.3
  213.7 0.6 dynamic-slice_bitcast_fusion.here_ref
  214.3 31.1 %branch_1_fun.5 = (bf16[1024,2560]{1,0:T(8,128)(2,1)}, bf16[8192,256]{1,0:T(8,128)(2,1)}, bf16[8192,256]{1,0:T(8,128)(2,1)}, bf16[8192,256]{1,0:T(8,128)(2,1)}) custom-call(s32[8192]{0:T(1024)} %copy-done.3, s32[8,128]{1,0:T(8,128)} %dynamic-slice_bitcast_fusion.here_ref, f32[8192,256]{1,0:T(8,128)} %get-tuple-element.109.rope_ref, ...), custom_call_target="tpu_custom_call" | custom-call | tf_op jit(solution)/shard_map/cond/branch_1_fun/pallas_call | solution.py:459
  (9 shorter events, 0.1 us)
Async XLA Ops:
  10.3 203.4 %copy-start.3 = (s32[8192]{0:T(1024)}, s32[8192]{0:T(1024)S(1)}, u32[]{:S(2)}) copy-start(s32[8192]{0:T(1024)S(1)} %get-tuple-element.141.idx_ref) | copy-start | bytes 98308 | tf_op jit(solution)/shard_map/cond
  13.0 11.7 %slice-start = ((s8[5242880]{0:T(1024)(128)(4,1)}), s8[4194304]{0:T(1024)(128)(4,1)S(1)}, s32[]{:S(2)}) async-start(s8[5242880]{0:T(1024)(128)(4,1)} %bitcast.48), calls=%async_computation.2 | async-start | bytes 8388608 | tf_op jit(solution)/shard_map/cond
  14.0 9.0 %copy-start.5 = (s32[8192]{0:T(1024)S(1)}, s32[8192]{0:T(1024)}, u32[]{:S(2)}) copy-start(s32[8192]{0:T(1024)} %get-tuple-element.104) | copy-start | bytes 98308 | tf_op jit(solution)/shard_map/cond
  14.0 9.6 %copy-start.7 = (f32[2560]{0:T(1024)S(1)}, f32[2560]{0:T(1024)}, u32[]{:S(2)}) copy-start(f32[2560]{0:T(1024)} %get-tuple-element.105) | copy-start | bytes 30724 | tf_op jit(solution)/shard_map/cond
  14.0 10.8 %slice-start.1 = ((s8[5242880]{0:T(1024)(128)(4,1)}), s8[1048576]{0:T(1024)(128)(4,1)S(1)}, s32[]{:S(2)}) async-start(s8[5242880]{0:T(1024)(128)(4,1)} %bitcast.48), calls=%async_computation.3 | async-start | bytes 2097152 | tf_op jit(solution)/shard_map/cond
  14.0 10.8 %copy-start.2 = (bf16[2560,256]{1,0:T(8,128)(2,1)S(1)}, bf16[2560,256]{1,0:T(8,128)(2,1)}, u32[]{:S(2)}) copy-start(bf16[2560,256]{1,0:T(8,128)(2,1)} %get-tuple-element.106.wq) | copy-start | bytes 3932164 | tf_op jit(solution)/shard_map/cond

commit v3 on v2

--- a/solution.py
+++ b/solution.py
@@ -9,26 +9,32 @@
 from jax.sharding import PartitionSpec as P
 
 HEAD_DIM = 256
+LANES = 128
 EPSILON = 1e-6
 ROPE_BASE = 10000.0
 MESH = pl.DeviceIdType.MESH
 
 HOT = 1024
-CH = 64
-CHIP_CHUNKS = (35, 6, 3, 3)
-DEV1_CHUNKS = 10
+CH = 32
+PRE = 12
+CHIP_CHUNKS = (57, 11, 6, 6)
+DEV1_CHUNKS = 19
 HOT_CHUNKS = HOT // CH
-RING_CHUNKS = sum(CHIP_CHUNKS)
+HOT_STREAM = HOT_CHUNKS - 2 * PRE
+RING_CHUNKS = PRE + sum(CHIP_CHUNKS)
 RING_ROWS = RING_CHUNKS * CH
 ROWS = 2 * RING_ROWS
-COLD0_CHUNKS = 2 * CHIP_CHUNKS[0] - DEV1_CHUNKS - HOT_CHUNKS
-CAPS = tuple(CH * n for n in (COLD0_CHUNKS, DEV1_CHUNKS, 6, 6, 3, 3, 3, 3))
-CAP = max(CAPS)
+COLD0_CHUNKS = 2 * CHIP_CHUNKS[0] - DEV1_CHUNKS - HOT_STREAM
+CAPS = tuple(CH * n for n in (COLD0_CHUNKS, DEV1_CHUNKS) + tuple(CHIP_CHUNKS[d // 2] for d in range(2, 8)))
+CAP = -(-max(CAPS) // LANES) * LANES
 RING_ORDER = ((0, 1, 3, 2), (0, 2, 3, 1))
-BLK = 128
+BLK = LANES
 NBLK = -(-RING_ROWS // BLK)
+ROPE = 2
+PER_TURN = BLK // CH // 2
 TILE = 128
 NTILE = CAP // TILE
+VOCAB_SHIFT = 15
 
 
 def _base_rows():
@@ -40,7 +46,7 @@
             pos, src = order.index(chip), order.index(owner)
             hops = (pos - src) % 4
             before = sum(CHIP_CHUNKS[order[(pos - k) % 4]] for k in range(hops))
-            base[chip, dev] = ring * RING_ROWS + before * CH
+            base[chip, dev] = ring * RING_ROWS + (PRE + before) * CH
     return base
 
 
@@ -60,10 +66,10 @@
 
 
 def pick_odd(rows_row, count):
-    odd = jnp.transpose(jnp.broadcast_to(rows_row & 1, (128, 128)))[:count, :]
-    row = lax.broadcasted_iota(jnp.int32, (count, 128), 0)
-    col = lax.broadcasted_iota(jnp.int32, (count, 128), 1)
-    halves = [jnp.where(col + part == 2 * row + odd, 1.0, 0.0) for part in range(0, 2 * count, 128)]
+    odd = jnp.transpose(jnp.broadcast_to(rows_row & 1, (LANES, LANES)))[:count, :]
+    row = lax.broadcasted_iota(jnp.int32, (count, LANES), 0)
+    col = lax.broadcasted_iota(jnp.int32, (count, LANES), 1)
+    halves = [jnp.where(col + part == 2 * row + odd, 1.0, 0.0) for part in range(0, 2 * count, LANES)]
     return jnp.concatenate(halves, axis=1).astype(jnp.bfloat16)
 
 
@@ -118,11 +124,211 @@
         scratch_shapes=[pltpu.VMEM((2 * CAP, width), jnp.bfloat16), pltpu.VMEM((CAP, width), jnp.bfloat16),
                         pltpu.SemaphoreType.DMA((NTILE,)), pltpu.SemaphoreType.DMA((NTILE,))],
         compiler_params=pltpu.CompilerParams(vmem_limit_bytes=60_000_000),
-    )(flat, flat.reshape(NTILE, TILE), table)
-
-
-def ring_kernel(packed, table, pos_ref, freq_ref, scale_ref, wq, wk, wv, lin_out, rows_out, rope_out,
-                rows, wbuf, nbuf, oblk, rope_buf, rsem, nsem, ssem, xsem, osem, ksem, psem, wsem):
+    )(flat.reshape(-1), flat, table)
+
+
+def place_tokens(dev, ids_ref, idx_ref, flat_ref, fits_ref, rank_s, high_s, low_s, list_s, off_s, count_s):
+    groups = ids_ref.shape[0]
+    f32, bf16 = jnp.float32, jnp.bfloat16
+    ids = ids_ref[...]
+    owner = lax.shift_right_logical(ids, VOCAB_SHIFT)
+    cold = ids >= HOT
+    chip = dev // 2
+
+    def square(n):
+        return lax.broadcasted_iota(jnp.int32, (n, n), 0), lax.broadcasted_iota(jnp.int32, (n, n), 1)
+
+    row, col = square(LANES)
+    earlier = jnp.where(row < col, 1.0, 0.0).astype(bf16)
+    ones = jnp.full((LANES, LANES), 1.0, bf16)
+    low_row, low_col = square(groups)
+    lower = jnp.where(low_col < low_row, 1.0, 0.0).astype(bf16)
+    base_rows = _base_rows()
+    base = []
+    for d in range(9):
+        value = jnp.int32(int(base_rows[0, d]))
+        for c in range(1, 4):
+            value = jnp.where(chip == c, int(base_rows[c, d]), value)
+        base.append(value)
+    rank = jnp.zeros((groups, LANES), f32)
+    place = jnp.zeros((groups, LANES), f32)
+    off_here, count_here = rank, rank
+    first = jnp.zeros((groups, LANES), jnp.int32)
+    over = jnp.zeros((1, LANES), f32)
+    for d in range(8):
+        held = cold & (owner == d)
+        flags = jnp.where(held, 1.0, 0.0).astype(bf16)
+        within = jnp.dot(flags, earlier, preferred_element_type=f32)
+        count = jnp.dot(flags, ones, preferred_element_type=f32)
+        off = jnp.dot(lower, count.astype(bf16), preferred_element_type=f32)
+        rank = jnp.where(held, off + within, rank)
+        first = jnp.where(held, base[d], first)
+        over = jnp.where((off + count)[groups - 1:, :] > float(CAPS[d]), 1.0, over)
+        place = jnp.where(dev == d, jnp.where(held, within, -1.0), place)
+        off_here = jnp.where(dev == d, off, off_here)
+        count_here = jnp.where(dev == d, count, count_here)
+    fits_ref[...] = jnp.broadcast_to(jnp.where(over > 0.0, 0, 1), (8, LANES))
+    ranks = rank.astype(jnp.int32)
+    early, split = PRE * CH, CHIP_CHUNKS[0] * CH
+    slot = jnp.where(cold, HOT + ranks, ids) - 2 * early
+    idx0 = jnp.where(slot < split, base[0] + slot, base[8] + DEV1_CHUNKS * CH + slot - split)
+    idx0 = jnp.where(ids < 2 * early, jnp.where(ids < early, ids, ids - early + RING_ROWS), idx0)
+    idx_ref[...] = jnp.where(owner == 0, idx0, first + ranks)
+
+    rank_s[...] = place
+    high_s[...] = (lax.shift_right_logical(ids, 8) & (2 ** (VOCAB_SHIFT - 8) - 1)).astype(f32)
+    low_s[...] = (ids & 255).astype(f32)
+    list_s[...] = jnp.zeros_like(list_s)
+    off_s[...] = jnp.zeros_like(off_s)
+    count_s[...] = jnp.zeros_like(count_s)
+    off_s[:groups, :] = off_here
+    count_s[:groups, :] = count_here
+    sub_row = lax.broadcasted_iota(jnp.int32, (8, LANES), 0)
+    row_f = row.astype(f32)
+
+    def compact(b, carry):
+        here = pl.ds(b, 1)
+        pick = jnp.where(rank_s[here, :] == row_f, 1.0, 0.0).astype(bf16)
+        digits = jnp.where(sub_row == 0, high_s[here, :], jnp.where(sub_row == 1, low_s[here, :], 0.0)).astype(bf16)
+        found = lax.dot_general(digits, pick, (((1,), (1,)), ((), ())), preferred_element_type=f32)
+        list_s[here, :] = found[0:1, :] * 256.0 + found[1:2, :]
+        return carry
+    lax.fori_loop(0, groups, compact, 0, unroll=4)
+
+    listed = jnp.transpose(list_s[...])
+    high = jnp.floor(listed * (1.0 / 256.0))
+    low = (listed - high * 256.0).astype(bf16)
+    high = high.astype(bf16)
+    flat_ref[...] = jnp.zeros_like(flat_ref)
+
+    def spread(i, carry):
+        at = (col + i * LANES).astype(f32)
+        mine = (off_s[...] <= at) & (at < off_s[...] + count_s[...])
+        group = jnp.where(mine, 1.0, 0.0).astype(bf16)
+        column = at[0:1, :] - jnp.sum(jnp.where(mine, off_s[...], 0.0), axis=0, keepdims=True)
+        value = (jnp.dot(high, group, preferred_element_type=f32) * 256.0
+                 + jnp.dot(low, group, preferred_element_type=f32))
+        value = jnp.sum(jnp.where(row_f == column, value, 0.0), axis=0, keepdims=True)
+        flat_ref[pl.ds(i, 1), :] = value.astype(jnp.int32)
+        return carry
+    lax.fori_loop(0, NTILE, spread, 0)
+
+
+def early_kernel(table, ids_ref, pre, idx_ref, flat_ref, fits_ref, rsem, nsem, ssem, *scratch):
+    dev = lax.axis_index("tp")
+
+    def tokens():
+        place_tokens(dev, ids_ref, idx_ref, flat_ref, fits_ref, *scratch)
+
+    chip, core = dev // 2, dev % 2
+    sib = chip * 2 + 1 - core
+    after = jnp.where(dev == 2, 6, jnp.where(dev == 6, 4, jnp.where(dev == 5, 7, 3)))
+    before = jnp.where(dev == 6, 2, jnp.where(dev == 4, 6, jnp.where(dev == 7, 5, jnp.where(dev == 3, 7, 1))))
+    ends = (dev == 3) | (dev == 4)
+    barrier = pltpu.get_barrier_semaphore()
+
+    def greet(other):
+        pl.semaphore_signal(barrier, inc=1, device_id={"tp": other}, device_id_type=MESH)
+
+    greet(sib)
+
+    @pl.when(dev == 1)
+    def _():
+        greet(2)
+        greet(5)
+
+    @pl.when(dev >= 2)
+    def _():
+        greet(before)
+
+    @pl.when((dev >= 2) & jnp.logical_not(ends))
+    def _():
+        greet(after)
+    pl.semaphore_wait(barrier, jnp.where(dev == 0, 1, jnp.where(ends, 2, 3)))
+
+    def chunk(ref, c):
+        return ref.at[pl.ds(_mo(c * CH, CH), CH), :]
+
+    def send(src, c, sem, to):
+        return pltpu.make_async_remote_copy(
+            src_ref=chunk(src, c), dst_ref=chunk(pre, c), send_sem=sem.at[c], recv_sem=rsem.at[c],
+            device_id={"tp": to}, device_id_type=MESH)
+
+    def arrive(c):
+        pltpu.make_async_copy(chunk(table, 0), chunk(pre, c), rsem.at[c]).wait()
+
+    def each(count, body):
+        def step(i, carry):
+            body(i)
+            return carry
+        lax.fori_loop(0, count, step, 0)
+
+    @pl.when(dev == 0)
+    def _():
+        def both(k):
+            for ring in range(2):
+                send(table, ring * PRE + k, ssem, sib).start()
+        each(PRE, both)
+        tokens()
+        each(2 * PRE, lambda c: send(table, c, ssem, sib).wait_send())
+
+    @pl.when(dev == 1)
+    def _():
+        def both(k):
+            for ring, to in ((0, 2), (1, 5)):
+                arrive(ring * PRE + k)
+                send(pre, ring * PRE + k, nsem, to).start()
+        each(PRE, both)
+        tokens()
+        each(2 * PRE, lambda c: send(pre, c, nsem, 2).wait_send())
+
+    @pl.when(dev >= 2)
+    def _():
+        def pass_on(k):
+            c = core * PRE + k
+            arrive(c)
+
+            @pl.when(jnp.logical_not(ends))
+            def _():
+                send(pre, c, nsem, after).start()
+            send(pre, c, ssem, sib).start()
+        late = (dev == 2) | (dev == 5)
+
+        @pl.when(jnp.logical_not(late))
+        def _():
+            tokens()
+        each(PRE, pass_on)
+
+        @pl.when(late)
+        def _():
+            tokens()
+        each(PRE, lambda k: arrive((1 - core) * PRE + k))
+        each(PRE, lambda k: send(pre, core * PRE + k, ssem, sib).wait_send())
+
+        @pl.when(jnp.logical_not(ends))
+        def _():
+            each(PRE, lambda k: send(pre, core * PRE + k, nsem, after).wait_send())
+
+
+def early_call(table, ids):
+    anywhere = pl.BlockSpec(memory_space=pl.ANY)
+    vmem = pl.BlockSpec(memory_space=pltpu.VMEM)
+    groups = ids.shape[0]
+    return pl.pallas_call(
+        early_kernel,
+        out_shape=(jax.ShapeDtypeStruct((2 * PRE * CH, table.shape[1]), table.dtype),
+                   jax.ShapeDtypeStruct((groups, LANES), jnp.int32),
+                   jax.ShapeDtypeStruct((-(-NTILE // 8) * 8, LANES), jnp.int32),
+                   jax.ShapeDtypeStruct((8, LANES), jnp.int32)),
+        in_specs=[anywhere, vmem], out_specs=(anywhere, vmem, vmem, vmem),
+        scratch_shapes=[pltpu.SemaphoreType.DMA((2 * PRE,))] * 3 + [pltpu.VMEM((groups, LANES), jnp.float32)] * 3
+        + [pltpu.VMEM((LANES, LANES), jnp.float32)] * 3,
+        compiler_params=pltpu.CompilerParams(collective_id=1, has_side_effects=True),
+    )(table, ids)
+
+
+def ring_kernel(packed, table, pre, pos_ref, freq_ref, scale_ref, wq, wk, wv, lin_out, rows_out, rope_out,
+                rows, wbuf, nbuf, oblk, obf, rope_buf, rsem, nsem, ssem, xsem, osem, ksem, psem, wsem):
     width = rows.shape[1]
     normalizer = float(np.asarray(math.sqrt(width), dtype=jnp.bfloat16))
     dev = lax.axis_index("tp")
@@ -142,6 +348,10 @@
     own = chunks_of(chip)
     n_next = chunks_of(next_chip)
     local = jnp.where(dev == 1, DEV1_CHUNKS, own)
+
+    def passed(u):
+        return PRE + local + (jnp.minimum(u, 2 * NBLK) * (RING_CHUNKS - PRE - local)) // (2 * NBLK)
+
     n_send = RING_CHUNKS - n_next
 
     barrier = pltpu.get_barrier_semaphore()
@@ -169,28 +379,44 @@
 
     def to_sib_other(i):
         return pltpu.make_async_remote_copy(
-            src_ref=chunk(1, i), dst_ref=chunk(1, i), send_sem=xsem.at[i - DEV1_CHUNKS],
+            src_ref=chunk(1, i), dst_ref=chunk(1, i), send_sem=xsem.at[i - PRE - DEV1_CHUNKS],
             recv_sem=sem_of(1, i), device_id={"tp": sib}, device_id_type=MESH)
 
+    def load_pre(i, carry):
+        for ring in range(2):
+            from_rows = pl.ds(_mo((ring * PRE + i) * CH, CH), CH)
+
+            @pl.when(dev == 0)
+            def _():
+                pltpu.make_async_copy(table.at[from_rows, :], chunk(ring, i), sem_of(ring, i)).start()
+
+            @pl.when(dev != 0)
+            def _():
+                pltpu.make_async_copy(pre.at[from_rows, :], chunk(ring, i), sem_of(ring, i)).start()
+        return carry
+
     def load(i, carry):
-        @pl.when((dev == 0) & (i < HOT_CHUNKS))
-        def _():
-            pltpu.make_async_copy(table.at[pl.ds(_mo(i * CH, CH), CH), :], chunk(core, i), sem_of(core, i)).start()
-
-        @pl.when((dev != 0) | (i >= HOT_CHUNKS))
-        def _():
-            first = i - jnp.where(dev == 0, HOT_CHUNKS, 0)
-            pltpu.make_async_copy(packed.at[pl.ds(_mo(first * CH, CH), CH), :], chunk(core, i), sem_of(core, i)).start()
+        to, sem = chunk(core, PRE + i), sem_of(core, PRE + i)
+
+        @pl.when((dev == 0) & (i < HOT_STREAM))
+        def _():
+            pltpu.make_async_copy(table.at[pl.ds(_mo((2 * PRE + i) * CH, CH), CH), :], to, sem).start()
+
+        @pl.when((dev != 0) | (i >= HOT_STREAM))
+        def _():
+            first = i - jnp.where(dev == 0, HOT_STREAM, 0)
+            pltpu.make_async_copy(packed.at[pl.ds(_mo(first * CH, CH), CH), :], to, sem).start()
         return carry
     lax.fori_loop(0, local, load, 0)
 
     @pl.when(dev == 0)
     def _():
         def load_other(i, carry):
-            first = i - DEV1_CHUNKS + CHIP_CHUNKS[0] - HOT_CHUNKS
-            pltpu.make_async_copy(packed.at[pl.ds(_mo(first * CH, CH), CH), :], chunk(1, i), sem_of(1, i)).start()
+            first = i - DEV1_CHUNKS + CHIP_CHUNKS[0] - HOT_STREAM
+            pltpu.make_async_copy(packed.at[pl.ds(_mo(first * CH, CH), CH), :], chunk(1, PRE + i), sem_of(1, PRE + i)).start()
             return carry
         lax.fori_loop(DEV1_CHUNKS, CHIP_CHUNKS[0], load_other, 0)
+    lax.fori_loop(0, PRE, load_pre, 0)
 
     weights = []
     for k, w in enumerate((wq, wk, wv)):
@@ -205,7 +431,7 @@
         wait_chunk(core, i)
         to_next(i).start()
         return carry
-    lax.fori_loop(0, local, first_sends, 0)
+    lax.fori_loop(PRE, PRE + local, first_sends, 0)
 
     @pl.when(dev == 0)
     def _():
@@ -213,32 +439,36 @@
             wait_chunk(1, i)
             to_sib_other(i).start()
             return carry
-        lax.fori_loop(DEV1_CHUNKS, CHIP_CHUNKS[0], send_other, 0)
+        lax.fori_loop(PRE + DEV1_CHUNKS, PRE + CHIP_CHUNKS[0], send_other, 0)
 
     def first_sib(i, carry):
         to_sib(i).start()
         return carry
-    lax.fori_loop(0, local, first_sib, 0)
-
+    lax.fori_loop(PRE, PRE + local, first_sib, 0)
+
+    def wait_pre(i, carry):
+        for ring in range(2):
+            wait_chunk(ring, i)
+        return carry
+    lax.fori_loop(0, PRE, wait_pre, 0)
     for copy in weights:
         copy.wait()
 
-    def relay(i):
-        @pl.when((i >= local) & (i < RING_CHUNKS))
-        def _():
-            wait_chunk(core, i)
-
-            @pl.when(i < n_send)
-            def _():
-                to_next(i).start()
-
-            @pl.when((dev != 1) | (i >= CHIP_CHUNKS[0]))
-            def _():
-                to_sib(i).start()
+    def relay(i, carry):
+        wait_chunk(core, i)
+
+        @pl.when(i < n_send)
+        def _():
+            to_next(i).start()
+
+        @pl.when((dev != 1) | (i >= PRE + CHIP_CHUNKS[0]))
+        def _():
+            to_sib(i).start()
+        return carry
 
     def lin_copy(first, slot):
         return pltpu.make_async_copy(
-            oblk.at[slot], lin_out.at[pl.ds(_mo(first * 8, CH * 8), BLK * 8), :], osem.at[slot])
+            obf.at[slot], lin_out.at[pl.ds(first, BLK), :, :], osem.at[slot])
 
     def keep_copy(first, slot):
         here = pl.ds(_mo(first, CH), BLK)
@@ -246,17 +476,17 @@
 
     def rope_copy(group, slot):
         return pltpu.make_async_copy(
-            rope_buf.at[slot], rope_out.at[pl.ds(_mo(group * 128, 128), 128), :], psem.at[slot])
+            rope_buf.at[slot], rope_out.at[pl.ds(_mo(group * LANES, LANES), LANES), :], psem.at[slot])
 
     def rope_tables_of(group, slot):
-        angle = jnp.transpose(jnp.broadcast_to(pos_ref[pl.ds(group, 1), :], (128, 128))) * freq_ref[...]
+        angle = jnp.transpose(jnp.broadcast_to(pos_ref[pl.ds(group, 1), :].astype(jnp.float32), (LANES, LANES))) * freq_ref[...]
         cosine, sine = cos_sin(angle)
 
         @pl.when(group >= 2)
         def _():
             rope_copy(group, slot).wait()
-        rope_buf[slot, :, :128] = cosine
-        rope_buf[slot, :, 128:] = sine
+        rope_buf[slot, :, :LANES] = cosine
+        rope_buf[slot, :, LANES:] = sine
         rope_copy(group, slot).start()
 
     def block_start(b):
@@ -281,35 +511,36 @@
         keep_copy(first, slot).start()
         for k in range(3):
             lin = jnp.dot(nbuf[...], wbuf[:, k * HEAD_DIM:(k + 1) * HEAD_DIM], preferred_element_type=jnp.float32)
-            lin = lin.astype(jnp.bfloat16).astype(jnp.float32)
             for half in range(2):
-                oblk[slot, pl.ds(2 * k + half, BLK, stride=8), :] = lin[:, half * 128:(half + 1) * 128]
+                oblk[pl.ds(2 * k + half, BLK, stride=8), :] = lin[:, half * LANES:(half + 1) * LANES]
+        obf[slot] = oblk[...].reshape(BLK, 8, LANES).astype(jnp.bfloat16)
         lin_copy(first, slot).start()
 
     def turn_body(u, carry):
         b, half = u // 2, u % 2
         turn = u - 2
         ring = jnp.where(half == 0, core, 1 - core)
-        relay(u)
+        lax.fori_loop(passed(u), passed(u + 1), relay, 0)
 
         @pl.when(turn >= 0)
         def _():
             @pl.when(half == 1)
             def _():
                 def wait_one(k, c):
-                    i = 2 * (b - 1) + k
-
-                    @pl.when((i < RING_CHUNKS) & ((dev != 0) | (i < DEV1_CHUNKS) | (i >= CHIP_CHUNKS[0])))
+                    i = 2 * PER_TURN * (b - 1) + k
+
+                    @pl.when((i >= PRE) & (i < RING_CHUNKS) &
+                             ((dev != 0) | (i < PRE + DEV1_CHUNKS) | (i >= PRE + CHIP_CHUNKS[0])))
                     def _():
                         wait_chunk(1 - core, i)
                     return c
-                lax.fori_loop(0, 2, wait_one, 0)
+                lax.fori_loop(0, 2 * PER_TURN, wait_one, 0)
             projections(ring, b - 1, half, turn)
 
-        @pl.when((b >= 2) & (b < 2 + pos_ref.shape[0] // 4))
-        def _():
-            for k in range(2):
-                rope_tables_of((u - 4) * 2 + k, k)
+        @pl.when((turn >= 0) & (turn * ROPE < pos_ref.shape[0]))
+        def _():
+            for k in range(ROPE):
+                rope_tables_of(turn * ROPE + k, k % 2)
         return carry
     lax.fori_loop(0, 2 * NBLK + 2, turn_body, 0)
 
@@ -321,42 +552,43 @@
     def drain_next(i, carry):
         to_next(i).wait_send()
         return carry
-    lax.fori_loop(0, n_send, drain_next, 0)
+    lax.fori_loop(PRE, n_send, drain_next, 0)
 
     def drain_sib(i, carry):
-        @pl.when((dev != 1) | (i < DEV1_CHUNKS) | (i >= CHIP_CHUNKS[0]))
+        @pl.when((dev != 1) | (i < PRE + DEV1_CHUNKS) | (i >= PRE + CHIP_CHUNKS[0]))
         def _():
             to_sib(i).wait_send()
         return carry
-    lax.fori_loop(0, RING_CHUNKS, drain_sib, 0)
+    lax.fori_loop(PRE, RING_CHUNKS, drain_sib, 0)
 
     @pl.when(dev == 0)
     def _():
         def drain_other(i, carry):
             to_sib_other(i).wait_send()
             return carry
-        lax.fori_loop(DEV1_CHUNKS, CHIP_CHUNKS[0], drain_other, 0)
-
-
-def ring_call(packed, table, positions, norm_scale, w_query, w_key, w_value):
+        lax.fori_loop(PRE + DEV1_CHUNKS, PRE + CHIP_CHUNKS[0], drain_other, 0)
+
+
+def ring_call(packed, table, pre, positions, norm_scale, w_query, w_key, w_value):
     width = table.shape[1]
     tokens = positions.shape[0]
-    freq = ROPE_BASE ** (-jnp.arange(0, HEAD_DIM, 2, dtype=jnp.float32) / HEAD_DIM)
+    freq = (ROPE_BASE ** (-np.arange(0, HEAD_DIM, 2) / HEAD_DIM)).astype(np.float32)[None, :]
     anywhere = pl.BlockSpec(memory_space=pl.ANY)
     vmem = pl.BlockSpec(memory_space=pltpu.VMEM)
     return pl.pallas_call(
         ring_kernel,
-        out_shape=(jax.ShapeDtypeStruct((ROWS * 8, 128), jnp.float32),
+        out_shape=(jax.ShapeDtypeStruct((ROWS, 8, LANES), jnp.bfloat16),
                    jax.ShapeDtypeStruct((ROWS, width), jnp.bfloat16),
                    jax.ShapeDtypeStruct((tokens, HEAD_DIM), jnp.float32)),
-        in_specs=[anywhere, anywhere, vmem, vmem, vmem, anywhere, anywhere, anywhere],
+        in_specs=[anywhere, anywhere, anywhere, vmem, vmem, vmem, anywhere, anywhere, anywhere],
         out_specs=(anywhere, anywhere, anywhere),
         scratch_shapes=[
             pltpu.VMEM((ROWS, width), jnp.bfloat16),
             pltpu.VMEM((width, 3 * HEAD_DIM), jnp.bfloat16),
             pltpu.VMEM((BLK, width), jnp.bfloat16),
-            pltpu.VMEM((2, BLK * 8, 128), jnp.float32),
-            pltpu.VMEM((2, 128, HEAD_DIM), jnp.float32),
+            pltpu.VMEM((BLK * 8, LANES), jnp.float32),
+            pltpu.VMEM((2, BLK, 8, LANES), jnp.bfloat16),
+            pltpu.VMEM((2, LANES, HEAD_DIM), jnp.float32),
             pltpu.SemaphoreType.DMA((2 * RING_CHUNKS,)),
             pltpu.SemaphoreType.DMA((RING_CHUNKS,)),
             pltpu.SemaphoreType.DMA((RING_CHUNKS,)),
@@ -367,7 +599,7 @@
             pltpu.SemaphoreType.DMA((3,)),
         ],
         compiler_params=pltpu.CompilerParams(collective_id=0, has_side_effects=True, vmem_limit_bytes=60_000_000),
-    )(packed, table, positions.astype(jnp.float32).reshape(tokens // 128, 128), freq[None, :], norm_scale[None, :],
+    )(packed, table, pre, positions.reshape(tokens // LANES, LANES), jnp.asarray(freq), norm_scale[None, :],
       w_query, w_key, w_value)
 
 
@@ -386,9 +618,9 @@
     return cosine, sine
 
 
-EXPAND = 512
+EXPAND = 1024
 SUB = 64
-SHARE = 64
+SHARE = 128
 LOADS = 8
 
 
@@ -406,11 +638,11 @@
     def take(tile, picked):
         for t in range(SUB):
             row = idx_ref[tile * SUB + t]
-            picked[8 * t:8 * t + 8, :] = table[pl.ds(_mo(row * 8, 8), 8), :]
+            picked[8 * t:8 * t + 8, :] = table[row].astype(jnp.float32)
 
     @pl.when(step == 0)
     def _():
-        copies = [pltpu.make_async_copy(lin.at[pl.ds(n * piece, piece), :], table.at[pl.ds(n * piece, piece), :],
+        copies = [pltpu.make_async_copy(lin.at[pl.ds(n * piece, piece)], table.at[pl.ds(n * piece, piece)],
                                         sem.at[n]) for n in range(LOADS)]
         for n, copy in enumerate(copies):
             copy.start(priority=n % 2)
@@ -424,15 +656,15 @@
 
     def rope(n, picked):
         here = pl.ds(_mo(n * SUB, SUB), SUB)
-        cosines, sines = rope_ref[here, :128], rope_ref[here, 128:]
+        cosines, sines = rope_ref[here, :LANES], rope_ref[here, LANES:]
         part = [picked[pl.ds(s, SUB, stride=8), :] for s in range(6)]
         factor = HEAD_DIM ** -0.5
-        q_ref[here, :128] = ((part[0] * cosines - part[1] * sines) * factor).astype(jnp.bfloat16)
-        q_ref[here, 128:] = ((part[1] * cosines + part[0] * sines) * factor).astype(jnp.bfloat16)
-        k_ref[here, :128] = (part[2] * cosines - part[3] * sines).astype(jnp.bfloat16)
-        k_ref[here, 128:] = (part[3] * cosines + part[2] * sines).astype(jnp.bfloat16)
-        v_ref[here, :128] = part[4].astype(jnp.bfloat16)
-        v_ref[here, 128:] = part[5].astype(jnp.bfloat16)
+        q_ref[here, :LANES] = ((part[0] * cosines - part[1] * sines) * factor).astype(jnp.bfloat16)
+        q_ref[here, LANES:] = ((part[1] * cosines + part[0] * sines) * factor).astype(jnp.bfloat16)
+        k_ref[here, :LANES] = (part[2] * cosines - part[3] * sines).astype(jnp.bfloat16)
+        k_ref[here, LANES:] = (part[3] * cosines + part[2] * sines).astype(jnp.bfloat16)
+        v_ref[here, :LANES] = part[4].astype(jnp.bfloat16)
+        v_ref[here, LANES:] = part[5].astype(jnp.bfloat16)
 
     def two_tiles(n, carry):
         tile = step * tiles + 2 * n
@@ -446,13 +678,12 @@
     share = pairs.at[pl.ds(_mo(step * 2 * SHARE, 2 * SHARE), 2 * SHARE), :]
     pltpu.make_async_copy(rows.at[pl.ds(0, 2 * SHARE), :], share, gsem.at[step]).wait()
     normalizer = float(np.asarray(math.sqrt(rows.shape[1]), dtype=jnp.bfloat16))
-    half = jnp.where(step % 2 == 0, here_ref[pl.ds(step // 2, 1), :], pltpu.roll(here_ref[pl.ds(step // 2, 1), :], 128 - SHARE, 1))
-    emb = jnp.dot(pick_odd(half, SHARE), share[...], preferred_element_type=jnp.float32)
+    emb = jnp.dot(pick_odd(here_ref[pl.ds(lax.axis_index("tp") * steps + step, 1), :], SHARE), share[...], preferred_element_type=jnp.float32)
     res_ref[...] = (emb * normalizer).astype(jnp.bfloat16)
 
 
-def expand(idx, idx_here, rope, lin, rows):
-    tokens, width = idx.shape[0], rows.shape[1]
+def expand(idx, rope, lin, rows):
+    tokens, width = idx.size, rows.shape[1]
     steps = tokens // EXPAND
     head = jax.ShapeDtypeStruct((tokens, HEAD_DIM), jnp.bfloat16)
     head_spec = pl.BlockSpec((EXPAND, HEAD_DIM), lambda i: (i, 0))
@@ -464,11 +695,11 @@
                   pl.BlockSpec((EXPAND, HEAD_DIM), lambda i: (i, 0)),
                   pl.BlockSpec(memory_space=pl.ANY), pl.BlockSpec(memory_space=pl.ANY)],
         out_specs=(pl.BlockSpec((SHARE, width), lambda i: (i, 0)), head_spec, head_spec, head_spec),
-        scratch_shapes=[pltpu.VMEM(lin.shape, jnp.float32), pltpu.VMEM((SUB * 8, 128), jnp.float32),
-                        pltpu.VMEM((SUB * 8, 128), jnp.float32), pltpu.VMEM((steps * 2 * SHARE, width), jnp.bfloat16),
+        scratch_shapes=[pltpu.VMEM(lin.shape, jnp.bfloat16), pltpu.VMEM((SUB * 8, LANES), jnp.float32),
+                        pltpu.VMEM((SUB * 8, LANES), jnp.float32), pltpu.VMEM((steps * 2 * SHARE, width), jnp.bfloat16),
                         pltpu.SemaphoreType.DMA((LOADS,)), pltpu.SemaphoreType.DMA((steps,))],
         compiler_params=pltpu.CompilerParams(vmem_limit_bytes=60_000_000),
-    )(idx, idx_here.reshape(-1, 128), rope, lin, rows)
+    )(idx.reshape(-1), idx, rope, lin, rows)
 
 
 def rope_tables(positions):
@@ -518,58 +749,16 @@
 
 
 def solution(mesh):
-    base_rows = _base_rows()
-
     def local_step(token_ids, positions, table_rows, norm_scale, w_query, w_key, w_value):
-        dev = lax.axis_index("tp")
-        vocab_rows, width = table_rows.shape
         tokens = token_ids.shape[0]
-        groups = tokens // 128
-        ids = token_ids.reshape(groups, 128)
-        owner = ids // vocab_rows
-        cold = ids >= HOT
-        mine8 = (owner[None] == jnp.arange(8, dtype=jnp.int32)[:, None, None]) & cold[None]
-        strict = jnp.asarray(np.triu(np.ones((128, 128)), 1), jnp.bfloat16)
-        rank8 = jnp.dot(mine8.astype(jnp.bfloat16).reshape(8 * groups, 128), strict,
-                        preferred_element_type=jnp.float32).reshape(8, groups, 128)
-        count8 = jnp.sum(mine8.astype(jnp.int32), axis=2)
-        offset8 = jnp.sum(jnp.where(np.tri(groups, groups, -1, dtype=bool)[None], count8[:, None, :], 0), axis=2)
-        total8 = jnp.sum(count8, axis=1)
-        fits = jnp.all(total8 <= jnp.asarray(CAPS, jnp.int32))
+        pre, idx, flat, fits = early_call(table_rows, token_ids.reshape(tokens // LANES, LANES))
 
         def fast(token_ids, positions, table_rows, norm_scale, w_query, w_key, w_value):
-            rank8i = rank8.astype(jnp.int32)
-            rank = jnp.sum(jnp.where(mine8, rank8i + offset8[:, :, None], 0), axis=0)
-            base = lax.dynamic_index_in_dim(jnp.asarray(base_rows), dev // 2, 0, keepdims=False)
-            first = jnp.sum(jnp.where(mine8, base[:8, None, None], 0), axis=0)
-            slot0 = jnp.where(cold, HOT + rank, ids)
-            split = CHIP_CHUNKS[0] * CH
-            idx0 = jnp.where(slot0 < split, base[0] + slot0, base[8] + DEV1_CHUNKS * CH + slot0 - split)
-            idx = jnp.where(owner == 0, idx0, first + rank).reshape(tokens)
-
-            mine = lax.dynamic_index_in_dim(mine8, dev, 0, keepdims=False)
-            within = lax.dynamic_index_in_dim(rank8i, dev, 0, keepdims=False)
-            offset = lax.dynamic_index_in_dim(offset8, dev, 0, keepdims=False)
-            count = lax.dynamic_index_in_dim(count8, dev, 0, keepdims=False)
-            lane = jnp.arange(128, dtype=jnp.int32)
-            place = jnp.where(mine, within, -1)
-            local = ids - dev * vocab_rows
-            listed = jnp.sum(jnp.where(place[:, None, :] == lane[None, :, None], local[:, None, :], 0), axis=2)
-            slot = jnp.arange(CAP, dtype=jnp.int32)[:, None]
-            group = (offset[None] <= slot) & (slot < (offset + count)[None])
-            digits = jnp.concatenate([listed // 256, listed % 256], axis=1).astype(jnp.bfloat16)
-            found = jnp.dot(group.astype(jnp.bfloat16), digits, preferred_element_type=jnp.float32)
-            found = (found[:, :128] * 256.0 + found[:, 128:]).astype(jnp.int32)
-            column = slot - jnp.sum(jnp.where(group, offset[None], 0), axis=1, keepdims=True)
-            flat = jnp.sum(jnp.where(column == lane[None], found, 0), axis=1)
-
             packed = pack_rows(flat, table_rows)
-            share = tokens // 8
-            idx_here = lax.dynamic_slice_in_dim(idx, dev * share, share)
-            lin, rows, rope = ring_call(packed, table_rows, positions, norm_scale, w_query, w_key, w_value)
-            return tuple(expand(idx, idx_here, rope, lin, rows))
-
-        outs = lax.cond(fits, fast, general, token_ids, positions, table_rows, norm_scale, w_query, w_key, w_value)
+            lin, rows, rope = ring_call(packed, table_rows, pre, positions, norm_scale, w_query, w_key, w_value)
+            return tuple(expand(idx, rope, lin, rows))
+
+        outs = lax.cond(fits[0, 0] > 0, fast, general, token_ids, positions, table_rows, norm_scale, w_query, w_key, w_value)
         residual, heads = outs[0], outs[1:]
         return (residual,) + tuple(h.reshape(tokens, 1, HEAD_DIM) for h in heads)
 

time: 247 us -> 218 us (0.88)
  Pallas kernels: 229 us -> 214 us
  other arithmetic: 9.95 us -> 0 us
    pallas_call x1 -> x2, Pallas kernels: 189 us -> 179 us  [the longest x1 146 us: ring_call(): pl.pallas_call(ring_kernel, out_shape=(jax.ShapeDtypeStruct((ROWS, 8, LAN...]
    pallas_call x1, Pallas kernels: 31.1 us -> 25.5 us  [expand(): pl.pallas_call(expand_kernel, grid=(steps,), out_shape=(jax.ShapeDtypeStr...]
    reduce_sum x7 -> x0, other arithmetic: 4.37 us -> none  [the longest x1 1.69 us: fast(): jnp.sum(jnp.where(place[:, None, :] == lane[None, :, None], local[:, None...]
where the time goes in v3:
time: 218 us; the launch traced here: 217 us
  Pallas kernels  214 us (98%)
    pallas_call x1, Pallas kernels, ring_call(): pl.pallas_call(ring_kernel, out_shape=(jax.ShapeDtypeStruct((ROWS, 8, LAN...  146 us
    pallas_call x1, Pallas kernels, early_call(): pl.pallas_call(early_kernel, out_shape=(jax.ShapeDtypeStruct((2 * PRE * C...  32.8 us
    pallas_call x1, Pallas kernels, expand(): pl.pallas_call(expand_kernel, grid=(steps,), out_shape=(jax.ShapeDtypeStr...  25.5 us
    pallas_call x1, Pallas kernels, pack_rows(): pl.pallas_call(pack_kernel, out_shape=jax.ShapeDtypeStruct((CAP, width),...  8.96 us

profile of v3, /device:TPU:6, one launch (start us, length us, event | category | flops | bytes accessed | tf_op | source)
XLA Modules:
  0.0 217.2 jit_solution(9315602171661655477)
XLA Ops:
  0.6 0.0 copy-start.2
  0.6 0.0 copy-start.5
  0.7 0.0 copy-start.6
  0.7 32.8 %shard_map.120 = (bf16[768,2560]{1,0:T(8,128)(2,1)}, s32[64,128]{1,0:T(8,128)S(1)}, s32[24,128]{1,0:T(8,128)S(1)}, s32[8,128]{1,0:T(8,128)}) custom-call(bf16[32768,2560]{1,0:T(8,128)(2,1)} %table.1, s32[64,128]{1,0:T(8,128)} %bitcast.29), custom_call_target="tpu_custom_call" | custom-call | tf_op jit(solution)/shard_map/pallas_call | solution.py:317
  33.5 1.2 slice.15
  35.3 0.0 copy-done.2
  35.4 0.0 copy-done.5
  35.4 0.0 copy-done.6
  35.4 181.7 %conditional.1 = (bf16[1024,2560]{1,0:T(8,128)(2,1)}, bf16[8192,1,256]{2,0,1:T(8,128)(2,1)}, bf16[8192,1,256]{2,0,1:T(8,128)(2,1)}, bf16[8192,1,256]{2,0,1:T(8,128)(2,1)}) conditional(s32[]{:T(128)} %bitcast.14, (s32[8192]{0:T(1024)S(1)}, bf16[32768,2560]{1,0:T(8,128)(2,1)}, f32[2560]{0:T(1024)}, bf16[2560,256]{1,0:T(8,128)(2,1)S(1)}, ...), branch_computations={%region_0.3_spmd, %region_3.4_spmd} | conditional | flops 32331853824 | bytes 863329408 | solution.py:761
  35.6 0.0 copy-start.10
  35.6 0.0 copy-start.1
  35.6 9.0 %branch_1_fun.3.packed = bf16[2816,2560]{1,0:T(8,128)(2,1)} custom-call(s32[3072]{0:T(1024)S(1)} %bitcast.32, s32[24,128]{1,0:T(8,128)S(1)} %get-tuple-element.49.rows_ref, bf16[32768,2560]{1,0:T(8,128)(2,1)} %get-tuple-element.50.table), custom_call_target="tpu_custom_call" | custom-call | tf_op jit(solution)/shard_map/cond/branch_1_fun/pallas_call | solution.py:118
  44.6 0.0 copy-done.10
  44.6 0.6 broadcast_in_dim.32.scale_ref
  45.2 0.0 copy-done.1
  45.2 146.3 %branch_1_fun.4 = (bf16[5888,8,128]{2,1,0:T(8,128)(2,1)}, bf16[5888,2560]{1,0:T(8,128)(2,1)}, f32[8192,256]{1,0:T(8,128)}) custom-call(bf16[2816,2560]{1,0:T(8,128)(2,1)} %branch_1_fun.3.packed, bf16[32768,2560]{1,0:T(8,128)(2,1)} %get-tuple-element.50.table, bf16[768,2560]{1,0:T(8,128)(2,1)} %get-tuple-element.51.pre, s32[64,128]{1,0:T(8,128)S(1)} %bitcast.31, ...), custom_call_target="tpu_custom_call" | custom-call | tf_op jit(solution)/shard_map/cond/branch_1_fun/pallas_call | solution.py:578
  191.6 25.5 %branch_1_fun.5 = (bf16[1024,2560]{1,0:T(8,128)(2,1)}, bf16[8192,256]{1,0:T(8,128)(2,1)}, bf16[8192,256]{1,0:T(8,128)(2,1)}, bf16[8192,256]{1,0:T(8,128)(2,1)}) custom-call(s32[8192]{0:T(1024)S(1)} %bitcast.30, s32[64,128]{1,0:T(8,128)S(1)} %get-tuple-element.48.here_ref, f32[8192,256]{1,0:T(8,128)} %get-tuple-element.58.rope_ref, ...), custom_call_target="tpu_custom_call" | custom-call | tf_op jit(solution)/shard_map/cond/branch_1_fun/pallas_call | solution.py:690
Async XLA Ops:
  0.6 34.7 %copy-start.2 = (bf16[2560,256]{1,0:T(8,128)(2,1)S(1)}, bf16[2560,256]{1,0:T(8,128)(2,1)}, u32[]{:S(2)}) copy-start(bf16[2560,256]{1,0:T(8,128)(2,1)} %param.14) | copy-start | bytes 3932164
  0.6 34.7 %copy-start.5 = (s32[8192]{0:T(1024)S(1)}, s32[8192]{0:T(1024)}, u32[]{:S(2)}) copy-start(s32[8192]{0:T(1024)} %param.10) | copy-start | bytes 98308
  0.7 34.7 %copy-start.6 = (s32[8192]{0:T(1024)S(1)}, s32[8192]{0:T(1024)}, u32[]{:S(2)}) copy-start(s32[8192]{0:T(1024)} %param.11) | copy-start | bytes 98308
  35.6 9.0 %copy-start.10 = (f32[2560]{0:T(1024)S(1)}, f32[2560]{0:T(1024)}, u32[]{:S(2)}) copy-start(f32[2560]{0:T(1024)} %get-tuple-element.54) | copy-start | bytes 30724 | tf_op jit(solution)/shard_map/cond
  35.6 9.6 %copy-start.1 = (bf16[2560,1024]{1,0:T(8,128)(2,1)S(1)}, bf16[2560,1024]{1,0:T(8,128)(2,1)}, u32[]{:S(2)}) copy-start(bf16[2560,1024]{1,0:T(8,128)(2,1)} %get-tuple-element.56.wk) | copy-start | bytes 15728644 | tf_op jit(solution)/shard_map/cond

commit v4 on v3

--- a/solution.py
+++ b/solution.py
@@ -619,7 +619,7 @@
 
 
 EXPAND = 1024
-SUB = 64
+SUB = 32
 SHARE = 128
 LOADS = 8
 

time: 218 us -> 216 us (level)
  Pallas kernels: 214 us -> 211 us
where the time goes in v4:
time: 216 us; the launch traced here: 215 us
  Pallas kernels  211 us (98%)
    pallas_call x1, Pallas kernels, ring_call(): pl.pallas_call(ring_kernel, out_shape=(jax.ShapeDtypeStruct((ROWS, 8, LAN...  145 us
    pallas_call x1, Pallas kernels, early_call(): pl.pallas_call(early_kernel, out_shape=(jax.ShapeDtypeStruct((2 * PRE * C...  32.8 us
    pallas_call x1, Pallas kernels, expand(): pl.pallas_call(expand_kernel, grid=(steps,), out_shape=(jax.ShapeDtypeStr...  23.9 us
    pallas_call x1, Pallas kernels, pack_rows(): pl.pallas_call(pack_kernel, out_shape=jax.ShapeDtypeStruct((CAP, width),...  8.89 us

profile of v4, /device:TPU:6, one launch (start us, length us, event | category | flops | bytes accessed | tf_op | source)
XLA Modules:
  0.0 214.6 jit_solution(8397988719147403468)
XLA Ops:
  0.6 0.0 copy-start.2
  0.6 0.0 copy-start.5
  0.7 0.0 copy-start.6
  0.7 32.8 %shard_map.120 = (bf16[768,2560]{1,0:T(8,128)(2,1)}, s32[64,128]{1,0:T(8,128)S(1)}, s32[24,128]{1,0:T(8,128)S(1)}, s32[8,128]{1,0:T(8,128)}) custom-call(bf16[32768,2560]{1,0:T(8,128)(2,1)} %table.1, s32[64,128]{1,0:T(8,128)} %bitcast.29), custom_call_target="tpu_custom_call" | custom-call | tf_op jit(solution)/shard_map/pallas_call | solution.py:317
  33.5 1.2 slice.15
  35.3 0.0 copy-done.2
  35.4 0.0 copy-done.5
  35.4 0.0 copy-done.6
  35.4 179.0 %conditional.1 = (bf16[1024,2560]{1,0:T(8,128)(2,1)}, bf16[8192,1,256]{2,0,1:T(8,128)(2,1)}, bf16[8192,1,256]{2,0,1:T(8,128)(2,1)}, bf16[8192,1,256]{2,0,1:T(8,128)(2,1)}) conditional(s32[]{:T(128)} %bitcast.14, (s32[8192]{0:T(1024)S(1)}, bf16[32768,2560]{1,0:T(8,128)(2,1)}, f32[2560]{0:T(1024)}, bf16[2560,256]{1,0:T(8,128)(2,1)S(1)}, ...), branch_computations={%region_0.3_spmd, %region_3.4_spmd} | conditional | flops 32331853824 | bytes 863329408 | solution.py:761
  35.6 0.0 copy-start.10
  35.6 0.0 copy-start.1
  35.6 8.9 %branch_1_fun.3.packed = bf16[2816,2560]{1,0:T(8,128)(2,1)} custom-call(s32[3072]{0:T(1024)S(1)} %bitcast.32, s32[24,128]{1,0:T(8,128)S(1)} %get-tuple-element.49.rows_ref, bf16[32768,2560]{1,0:T(8,128)(2,1)} %get-tuple-element.50.table), custom_call_target="tpu_custom_call" | custom-call | tf_op jit(solution)/shard_map/cond/branch_1_fun/pallas_call | solution.py:118
  44.5 0.0 copy-done.10
  44.5 0.6 broadcast_in_dim.32.scale_ref
  45.2 0.0 copy-done.1
  45.2 145.3 %branch_1_fun.4 = (bf16[5888,8,128]{2,1,0:T(8,128)(2,1)}, bf16[5888,2560]{1,0:T(8,128)(2,1)}, f32[8192,256]{1,0:T(8,128)}) custom-call(bf16[2816,2560]{1,0:T(8,128)(2,1)} %branch_1_fun.3.packed, bf16[32768,2560]{1,0:T(8,128)(2,1)} %get-tuple-element.50.table, bf16[768,2560]{1,0:T(8,128)(2,1)} %get-tuple-element.51.pre, s32[64,128]{1,0:T(8,128)S(1)} %bitcast.31, ...), custom_call_target="tpu_custom_call" | custom-call | tf_op jit(solution)/shard_map/cond/branch_1_fun/pallas_call | solution.py:578
  190.4 23.9 %branch_1_fun.5 = (bf16[1024,2560]{1,0:T(8,128)(2,1)}, bf16[8192,256]{1,0:T(8,128)(2,1)}, bf16[8192,256]{1,0:T(8,128)(2,1)}, bf16[8192,256]{1,0:T(8,128)(2,1)}) custom-call(s32[8192]{0:T(1024)S(1)} %bitcast.30, s32[64,128]{1,0:T(8,128)S(1)} %get-tuple-element.48.here_ref, f32[8192,256]{1,0:T(8,128)} %get-tuple-element.58.rope_ref, ...), custom_call_target="tpu_custom_call" | custom-call | tf_op jit(solution)/shard_map/cond/branch_1_fun/pallas_call | solution.py:690
Async XLA Ops:
  0.6 34.7 %copy-start.2 = (bf16[2560,256]{1,0:T(8,128)(2,1)S(1)}, bf16[2560,256]{1,0:T(8,128)(2,1)}, u32[]{:S(2)}) copy-start(bf16[2560,256]{1,0:T(8,128)(2,1)} %param.14) | copy-start | bytes 3932164
  0.6 34.7 %copy-start.5 = (s32[8192]{0:T(1024)S(1)}, s32[8192]{0:T(1024)}, u32[]{:S(2)}) copy-start(s32[8192]{0:T(1024)} %param.10) | copy-start | bytes 98308
  0.7 34.7 %copy-start.6 = (s32[8192]{0:T(1024)S(1)}, s32[8192]{0:T(1024)}, u32[]{:S(2)}) copy-start(s32[8192]{0:T(1024)} %param.11) | copy-start | bytes 98308
  35.6 8.9 %copy-start.10 = (f32[2560]{0:T(1024)S(1)}, f32[2560]{0:T(1024)}, u32[]{:S(2)}) copy-start(f32[2560]{0:T(1024)} %get-tuple-element.54) | copy-start | bytes 30724 | tf_op jit(solution)/shard_map/cond
  35.6 9.5 %copy-start.1 = (bf16[2560,1024]{1,0:T(8,128)(2,1)S(1)}, bf16[2560,1024]{1,0:T(8,128)(2,1)}, u32[]{:S(2)}) copy-start(bf16[2560,1024]{1,0:T(8,128)(2,1)} %get-tuple-element.56.wk) | copy-start | bytes 15728644 | tf_op jit(solution)/shard_map/cond
